TPU v7x, 8 devices: a whole 2x2x1 slice. The times are simulated.
8 devices in a mesh: dp: 2 (over z, y), cp: 4 (over x, core).
Axes of the slice: x: 2, y: 2, z: 1, core: 2. Of those that a mesh axis runs over, the one named last changes fastest.
Arguments:
- hidden: bfloat16 [32, 512, 3584], P('dp', 'cp'), parts along dimension 0
- positions: int32 [32, 512], P('dp', 'cp'), parts along dimension 0
- norm_gain: bfloat16 [3584], replicated
- w_query: bfloat16 [3584, 3584], replicated
- w_key: bfloat16 [3584, 512], replicated
- w_value: bfloat16 [3584, 512], replicated
- w_out: bfloat16 [28, 128, 3584], replicated
Outputs:
- output: bfloat16 [32, 512, 3584], P('dp', 'cp'), parts along dimension 0
There are 2 independent parts. A program takes and returns all parts, laid end to end along the dimension named above; an argument that names none is the same for every part.
All inputs are finite; a program needn't handle non-finite values.
Results may differ from a plain program's by a relative error of at most 0.0074385.
Values are sent between devices in bfloat16 or wider.
A program may use at most 1 GiB of HBM per device.

v0:
```python
import jax
import jax.numpy as jnp
from jax import lax
from jax.sharding import PartitionSpec as P


def rms_norm(hidden, norm_gain):
    x_f32 = hidden.astype(jnp.float32)
    inv_rms = lax.rsqrt(jnp.mean(x_f32 * x_f32, axis=-1, keepdims=True) + 1e-5)
    return (x_f32 * inv_rms * norm_gain.astype(jnp.float32)).astype(jnp.bfloat16)


def rotary(proj_f32, positions):
    head_dim = proj_f32.shape[-1]
    half_dim = head_dim // 2
    inv_freq = 10000.0 ** (-2.0 * jnp.arange(half_dim, dtype=jnp.float32) / head_dim)
    angles = positions.astype(jnp.float32)[:, :, None] * inv_freq
    cos_part = jnp.cos(angles)[:, :, None, :]
    sin_part = jnp.sin(angles)[:, :, None, :]
    first_half = proj_f32[..., :half_dim]
    second_half = proj_f32[..., half_dim:]
    return jnp.concatenate([first_half * cos_part - second_half * sin_part, second_half * cos_part + first_half * sin_part], axis=-1).astype(jnp.bfloat16)


def attend_block(q_grp, k_blk, v_blk, att_state, allowed):
    run_max, run_sum, acc_out = att_state
    scores = jnp.einsum('bqkgd,bskd->bkgqs', q_grp, k_blk, preferred_element_type=jnp.float32) * (q_grp.shape[-1] ** -0.5)
    if allowed is not None:
        scores = jnp.where(allowed, scores, -jnp.inf)
    new_max = jnp.maximum(run_max, jnp.max(scores, axis=-1))
    prob_blk = jnp.exp(scores - new_max[..., None])
    rescale = jnp.exp(run_max - new_max)
    new_sum = run_sum * rescale + jnp.sum(prob_blk, axis=-1)
    new_acc = acc_out * rescale[..., None] + jnp.einsum('bkgqs,bskd->bkgqd', prob_blk, v_blk, preferred_element_type=jnp.float32)
    return new_max, new_sum, new_acc


def solution(mesh):
    n_cp = mesh.shape['cp']
    shift_pairs = [(src_dev, (src_dev + 1) % n_cp) for src_dev in range(n_cp)]

    def local_block(hidden, positions, norm_gain, w_query, w_key, w_value, w_out):
        batch_loc, seq_loc, model_dim = hidden.shape
        n_heads, head_dim, _ = w_out.shape
        n_kv = w_key.shape[1] // head_dim
        n_groups = n_heads // n_kv
        normed = rms_norm(hidden, norm_gain)
        q_rot = rotary(jnp.einsum('bsd,de->bse', normed, w_query, preferred_element_type=jnp.float32).reshape(batch_loc, seq_loc, n_heads, head_dim), positions)
        k_rot = rotary(jnp.einsum('bsd,de->bse', normed, w_key, preferred_element_type=jnp.float32).reshape(batch_loc, seq_loc, n_kv, head_dim), positions)
        v_loc = jnp.einsum('bsd,de->bse', normed, w_value, preferred_element_type=jnp.float32).astype(jnp.bfloat16).reshape(batch_loc, seq_loc, n_kv, head_dim)
        q_grp = q_rot.reshape(batch_loc, seq_loc, n_kv, n_groups, head_dim)
        my_index = lax.axis_index('cp')
        token_idx = jnp.arange(seq_loc)
        diag_mask = token_idx[:, None] >= token_idx[None, :]
        start_state = (
            jnp.full((batch_loc, n_kv, n_groups, seq_loc), -jnp.inf, jnp.float32),
            jnp.zeros((batch_loc, n_kv, n_groups, seq_loc), jnp.float32),
            jnp.zeros((batch_loc, n_kv, n_groups, seq_loc, head_dim), jnp.float32),
        )
        att_state = attend_block(q_grp, k_rot, v_loc, start_state, diag_mask)

        def step_fn(step_idx, loop_state):
            k_blk, v_blk, att_prev = loop_state
            k_blk, v_blk = lax.ppermute((k_blk, v_blk), 'cp', shift_pairs)
            src_block = (my_index - step_idx) % n_cp
            att_next = lax.cond(src_block < my_index, lambda state_kept: attend_block(q_grp, k_blk, v_blk, state_kept, None), lambda state_kept: state_kept, att_prev)
            return k_blk, v_blk, att_next

        _, _, final_state = lax.fori_loop(1, n_cp, step_fn, (k_rot, v_loc, att_state))
        run_max, run_sum, acc_out = final_state
        attn_out = (acc_out / run_sum[..., None]).astype(jnp.bfloat16)
        proj_out = jnp.einsum('bkgqd,kgde->bqe', attn_out, w_out.reshape(n_kv, n_groups, head_dim, model_dim), preferred_element_type=jnp.float32)
        return (hidden.astype(jnp.float32) + proj_out).astype(jnp.bfloat16)

    act_spec = P('dp', 'cp', None)
    return jax.shard_map(local_block, mesh=mesh, in_specs=(act_spec, P('dp', 'cp'), P(), P(), P(), P(), P()), out_specs=act_spec, check_vma=False)
```

profile of v0, /device:TPU:3, one launch (start us, length us, event | category | flops | bytes accessed | tf_op | source)
XLA Modules:
  0.0 651.7 jit_solution(14627349478470132466)
XLA Ops:
  0.0 0.0 copy-start.1
  0.0 8.1 %fusion.12 = f32[16,128]{1,0:T(8,128)S(1)} fusion(bf16[16,128,3584]{2,1,0:T(8,128)(2,1)} %param.11), kind=kLoop, calls=%fused_computation.17 | loop fusion | flops 22018048 | bytes 14688256 | tf_op jit(solution)/shard_map/reduce_sum | solution.py:9
  8.1 0.0 copy-done.1
  8.1 13.7 %fusion.30 = f32[16,128,512]{2,1,0:T(8,128)} fusion(bf16[16,128,3584]{2,1,0:T(8,128)(2,1)} %param.11, f32[3584]{0:T(1024)S(1)} %convert_element_type.37, f32[16,128]{1,0:T(8,128)S(1)} %add_rsqrt_fusion, bf16[3584,512]{1,0:T(8,128)(2,1)} %param.15), kind=kOutput, calls=%fused_computation.40 | convolution fusion | flops 7545552896 | bytes 22566912 | tf_op jit(solution)/shard_map/bsd,de->bse/dot_general | solution.py:49
  21.8 0.0 copy-start.2
  21.8 5.3 reshape.43
  27.1 6.1 fusion.45
  33.2 0.0 copy-done.2
  33.2 3.7 multiply_cosine_fusion
  36.9 1.5 subtract_convert_fusion.1
  38.5 2.5 pad_maximum_fusion.1
  40.9 67.9 %fusion.18 = f32[16,128,3584]{1,2,0:T(8,128)} fusion(bf16[3584,3584]{1,0:T(8,128)(2,1)} %param.14, bf16[16,128,3584]{2,1,0:T(8,128)(2,1)} %param.11, f32[3584]{0:T(1024)S(1)} %convert_element_type.37, f32[16,128]{1,0:T(8,128)S(1)} %add_rsqrt_fusion), kind=kOutput, calls=%fused_computation.26 | convolution fusion | flops 52642709504 | bytes 69752832 | tf_op jit(solution)/shard_map/bsd,de->bse/dot_general | solution.py:48
  108.8 0.3 copy.22
  109.1 0.3 copy.23
  109.4 15.2 %subtract_convert_fusion = (bf16[16,128,28,64]{1,3,2,0:T(8,128)(2,1)}, bf16[16,128,28,64]{1,3,2,0:T(8,128)(2,1)}) fusion(f32[16,128,28,128]{1,3,2,0:T(8,128)} %bitcast.81, f32[16,128,64]{1,2,0:T(8,128)S(1)} %copy.23, f32[16,128,64]{1,2,0:T(8,128)S(1)} %copy.22), kind=kLoop, calls=%fused_computation.37 | loop fusion | flops 29360128 | bytes 45088768 | tf_op jit(solution)/shard_map/convert.3
  124.6 13.8 %copy.24 = bf16[16,128,28,64]{3,1,2,0:T(8,128)(2,1)} copy(bf16[16,128,28,64]{1,3,2,0:T(8,128)(2,1)} %get-tuple-element.285) | data formatting | bytes 14680064 | tf_op jit(solution)/shard_map/convert.3
  138.5 13.8 %copy.25 = bf16[16,128,28,64]{3,1,2,0:T(8,128)(2,1)} copy(bf16[16,128,28,64]{1,3,2,0:T(8,128)(2,1)} %get-tuple-element.286) | data formatting | bytes 14680064 | tf_op jit(solution)/shard_map/convert.2
  152.3 19.6 %pad_maximum_fusion = bf16[16,128,4,7,128]{4,1,3,2,0:T(8,128)(2,1)} fusion(bf16[16,128,4,7,64]{4,1,3,2,0:T(8,128)(2,1)} %bitcast.80, bf16[16,128,4,7,64]{4,1,3,2,0:T(8,128)(2,1)} %bitcast.79), kind=kLoop, calls=%fused_computation.30 | loop fusion | flops 29360128 | bytes 29360128 | tf_op jit(solution)/shard_map/concatenate | solution.py:22
  171.9 15.4 %fusion.20 = (f32[16,4,7,128]{3,2,1,0:T(8,128)S(1)}, f32[16,4,128,128,7]{3,2,4,1,0:T(8,128)}) fusion(pred[128,128]{0,1:T(8,128)(4,1)S(1)} %iota_compare_fusion, bf16[16,128,4,7,128]{4,1,3,2,0:T(8,128)(2,1)} %pad_maximum_fusion, bf16[16,128,4,128]{3,1,2,0:T(8,128)(2,1)} %pad_maximum_fusion.1), kind=kOutput, calls=%fused_computation.28 | convolution fusion | flops 1901010944 | bytes 46383104 | tf_op jit(solution)/shard_map/bqkgd,bskd->bkgqs/dot_general | solution.py:27
  187.2 0.0 copy-start.3
  187.2 13.4 %fusion.17 = f32[16,4,7,128]{3,2,1,0:T(8,128)S(1)} fusion(f32[16,4,128,128,7]{3,2,4,1,0:T(8,128)} %get-tuple-element.296, f32[16,4,7,128]{3,2,1,0:T(8,128)S(1)} %get-tuple-element.361, pred[128,128]{0,1:T(8,128)(4,1)S(1)} %iota_compare_fusion), kind=kLoop, calls=%fused_computation.25 | loop fusion | flops 29302784 | bytes 29835264 | tf_op jit(solution)/shard_map/reduce_sum | solution.py:33
  200.6 0.1 exponential_multiply_fusion
  200.7 0.0 copy-done.3
  200.7 12.5 %fusion.37 = bf16[16,128,512]{2,1,0:T(8,128)(2,1)} fusion(bf16[3584,512]{1,0:T(8,128)(2,1)S(1)} %copy-done.3, bf16[16,128,3584]{2,1,0:T(8,128)(2,1)} %param.11, f32[3584]{0:T(1024)S(1)} %convert_element_type.37, f32[16,128]{1,0:T(8,128)S(1)} %add_rsqrt_fusion), kind=kOutput, calls=%fused_computation.50 | convolution fusion | flops 7546601472 | bytes 20469760 | tf_op jit(solution)/shard_map/bsd,de->bse/dot_general | solution.py:50
  213.2 2.5 reshape.44
  215.8 0.0 copy-start
  215.8 27.2 %broadcast_add_fusion = f32[16,4,7,128,128]{4,3,2,1,0:T(8,128)} fusion(f32[16,4,7,128]{3,2,1,0:T(8,128)S(1)} %get-tuple-element.291, f32[16,4,128,128,7]{3,2,4,1,0:T(8,128)} %get-tuple-element.296, f32[16,4,7,128]{3,2,1,0:T(8,128)S(1)} %get-tuple-element.361, pred[128,128]{0,1:T(8,128)(4,1)S(1)} %iota_compare_fusion, ...), kind=kOutput, calls=%fused_computation.32 | convolution fusion | flops 1908408320 | bytes 61292544 | tf_op jit(solution)/shard_map/bkgqs,bskd->bkgqd/dot_general | solution.py:34
  243.0 0.0 copy-done
  243.0 1.9 copy_bitcast_fusion
  244.9 335.4 %while.23 = (s32[]{:T(128)}, bf16[16,128,4,128]{3,1,2,0:T(8,128)(2,1)}, bf16[16,128,4,128]{3,1,2,0:T(8,128)(2,1)}, f32[16,4,7,128]{3,2,1,0:T(8,128)S(1)}, f32[16...) while((s32[]{:T(128)}, ...), condition=%wide.region_8.9_spmd, body=%wide.region_3.8_spmd.sunk | while | flops 3824271360 | bytes 194511280 | solution.py:69
  244.9 0.0 collective-permute-start
  244.9 0.0 collective-permute-start.1
  244.9 23.0 %collective-permute-done = bf16[16,128,4,128]{3,1,2,0:T(8,128)(2,1)S(1)} collective-permute-done((bf16[16,128,4,128]{3,1,2,0:T(8,128)(2,1)}, bf16[16,128,4,128]{3,1,2,0:T(8,128)(2,1)S(1)}, u32[]{:S(2)}, u32[]{:S(2)}) %collective-permute-start) | collective-permute-done | bytes 2097184 | tf_op jit(solution)/shard_map/while/body/eval_jaxpr/ppermute | solution.py:64
  267.8 22.5 %collective-permute-done.1 = bf16[16,128,4,128]{3,1,2,0:T(8,128)(2,1)} collective-permute-done((bf16[16,128,4,128]{3,1,2,0:T(8,128)(2,1)}, bf16[16,128,4,128]{3,1,2,0:T(8,128)(2,1)}, u32[]{:S(2)}, u32[]{:S(2)}) %collective-permute-start.1) | collective-permute-done | bytes 2097184 | tf_op jit(solution)/shard_map/while/body/eval_jaxpr/ppermute | solution.py:64
  290.3 61.9 %conditional.2 = ((f32[16,4,7,128]{3,2,1,0:T(8,128)S(1)}, f32[16,4,7,128]{3,2,1,0:T(8,128)S(1)}, f32[16,4,7,128,128]{4,3,2,1,0:T(8,128)})) conditional(s32[]{:T(128)} %convert_element_type.80, (f32[16,4,7,128]{3,2,1,0:T(8,128)S(1)}, f32[16,4,7,128]{3,2,1,0:T(8,128)S(1)}, f32[16,4,7,128,128]{4,3,2,1,0:T(8,128)}) %tuple.55, ...), branch_computations={%region_4.4_spmd, %region_5.7_spmd} | conditional | flops 3824271360 | bytes 169345056 | solution.py:66
  290.3 15.0 %bitcast_reduce_fusion = (f32[16,4,7,128]{3,2,1,0:T(8,128)S(1)}, f32[16,4,128,128,7]{3,2,4,1,0:T(8,128)}) fusion(bf16[16,128,4,7,128]{4,1,3,2,0:T(8,128)(2,1)} %get-tuple-element.229, bf16[16,128,4,128]{3,1,2,0:T(8,128)(2,1)S(1)} %get-tuple-element.228), kind=kOutput, calls=%fused_computation.1 | convolution fusion | flops 1893670912 | bytes 46366720 | tf_op jit(solution)/shard_map/while/body/eval_jaxpr/cond/branch_1_fun/bqkgd,bskd->bkgqs/dot_general | solution.py:27
  305.3 13.0 %fusion.3 = f32[16,4,7,128]{3,2,1,0:T(8,128)S(1)} fusion(f32[16,4,128,128,7]{3,2,4,1,0:T(8,128)} %get-tuple-element.284, f32[16,4,7,128]{3,2,1,0:T(8,128)S(1)} %max.2), kind=kLoop, calls=%fused_computation.5 | loop fusion | flops 21962752 | bytes 29818880 | tf_op jit(solution)/shard_map/while/body/eval_jaxpr/cond/branch_1_fun/reduce_sum | solution.py:33
  318.3 0.2 multiply_add_fusion.1
  318.5 33.7 %multiply_add_fusion = f32[16,4,7,128,128]{4,3,2,1,0:T(8,128)} fusion(f32[16,4,7,128,128]{4,3,2,1,0:T(8,128)} %get-tuple-element.231, f32[16,4,7,128]{3,2,1,0:T(8,128)S(1)} %get-tuple-element.282, f32[16,4,128,128,7]{3,2,4,1,0:T(8,128)} %get-tuple-element.284, f32[16,4,7,128]{3,2,1,0:T(8,128)S(1)} %max.2, bf16[16,128,4,128]{3,1,2,0:T(8,128)(2,1)} %get-tuple-element.232), kind=kOutput, calls=%fused_computation.3 | convolution fusion | flops 1908408320 | bytes 90636288 | tf_op jit(solution)/shard_map/while/body/eval_jaxpr/cond/branch_1_fun/bkgqs,bskd->bkgqd/dot_general | solution.py:34
  352.2 1.3 copy.75
  353.5 3.2 copy.76
  356.7 0.0 collective-permute-start
  356.7 2.4 collective-permute-start.1
  359.1 20.5 %collective-permute-done = bf16[16,128,4,128]{3,1,2,0:T(8,128)(2,1)S(1)} collective-permute-done((bf16[16,128,4,128]{3,1,2,0:T(8,128)(2,1)}, bf16[16,128,4,128]{3,1,2,0:T(8,128)(2,1)S(1)}, u32[]{:S(2)}, u32[]{:S(2)}) %collective-permute-start) | collective-permute-done | bytes 2097184 | tf_op jit(solution)/shard_map/while/body/eval_jaxpr/ppermute | solution.py:64
  379.6 22.5 %collective-permute-done.1 = bf16[16,128,4,128]{3,1,2,0:T(8,128)(2,1)} collective-permute-done((bf16[16,128,4,128]{3,1,2,0:T(8,128)(2,1)}, bf16[16,128,4,128]{3,1,2,0:T(8,128)(2,1)}, u32[]{:S(2)}, u32[]{:S(2)}) %collective-permute-start.1) | collective-permute-done | bytes 2097184 | tf_op jit(solution)/shard_map/while/body/eval_jaxpr/ppermute | solution.py:64
  402.1 61.9 %conditional.2 = ((f32[16,4,7,128]{3,2,1,0:T(8,128)S(1)}, f32[16,4,7,128]{3,2,1,0:T(8,128)S(1)}, f32[16,4,7,128,128]{4,3,2,1,0:T(8,128)})) conditional(s32[]{:T(128)} %convert_element_type.80, (f32[16,4,7,128]{3,2,1,0:T(8,128)S(1)}, f32[16,4,7,128]{3,2,1,0:T(8,128)S(1)}, f32[16,4,7,128,128]{4,3,2,1,0:T(8,128)}) %tuple.55, ...), branch_computations={%region_4.4_spmd, %region_5.7_spmd} | conditional | flops 3824271360 | bytes 169345056 | solution.py:66
  402.1 15.0 %bitcast_reduce_fusion = (f32[16,4,7,128]{3,2,1,0:T(8,128)S(1)}, f32[16,4,128,128,7]{3,2,4,1,0:T(8,128)}) fusion(bf16[16,128,4,7,128]{4,1,3,2,0:T(8,128)(2,1)} %get-tuple-element.229, bf16[16,128,4,128]{3,1,2,0:T(8,128)(2,1)S(1)} %get-tuple-element.228), kind=kOutput, calls=%fused_computation.1 | convolution fusion | flops 1893670912 | bytes 46366720 | tf_op jit(solution)/shard_map/while/body/eval_jaxpr/cond/branch_1_fun/bqkgd,bskd->bkgqs/dot_general | solution.py:27
  417.1 13.0 %fusion.3 = f32[16,4,7,128]{3,2,1,0:T(8,128)S(1)} fusion(f32[16,4,128,128,7]{3,2,4,1,0:T(8,128)} %get-tuple-element.284, f32[16,4,7,128]{3,2,1,0:T(8,128)S(1)} %max.2), kind=kLoop, calls=%fused_computation.5 | loop fusion | flops 21962752 | bytes 29818880 | tf_op jit(solution)/shard_map/while/body/eval_jaxpr/cond/branch_1_fun/reduce_sum | solution.py:33
  430.1 0.2 multiply_add_fusion.1
  430.3 33.7 %multiply_add_fusion = f32[16,4,7,128,128]{4,3,2,1,0:T(8,128)} fusion(f32[16,4,7,128,128]{4,3,2,1,0:T(8,128)} %get-tuple-element.231, f32[16,4,7,128]{3,2,1,0:T(8,128)S(1)} %get-tuple-element.282, f32[16,4,128,128,7]{3,2,4,1,0:T(8,128)} %get-tuple-element.284, f32[16,4,7,128]{3,2,1,0:T(8,128)S(1)} %max.2, bf16[16,128,4,128]{3,1,2,0:T(8,128)(2,1)} %get-tuple-element.232), kind=kOutput, calls=%fused_computation.3 | convolution fusion | flops 1908408320 | bytes 90636288 | tf_op jit(solution)/shard_map/while/body/eval_jaxpr/cond/branch_1_fun/bkgqs,bskd->bkgqd/dot_general | solution.py:34
  464.0 1.3 copy.75
  465.3 3.2 copy.76
  468.5 0.0 collective-permute-start
  468.5 0.0 collective-permute-start.1
  468.5 23.0 %collective-permute-done = bf16[16,128,4,128]{3,1,2,0:T(8,128)(2,1)S(1)} collective-permute-done((bf16[16,128,4,128]{3,1,2,0:T(8,128)(2,1)}, bf16[16,128,4,128]{3,1,2,0:T(8,128)(2,1)S(1)}, u32[]{:S(2)}, u32[]{:S(2)}) %collective-permute-start) | collective-permute-done | bytes 2097184 | tf_op jit(solution)/shard_map/while/body/eval_jaxpr/ppermute | solution.py:64
  491.4 22.5 %collective-permute-done.1 = bf16[16,128,4,128]{3,1,2,0:T(8,128)(2,1)} collective-permute-done((bf16[16,128,4,128]{3,1,2,0:T(8,128)(2,1)}, bf16[16,128,4,128]{3,1,2,0:T(8,128)(2,1)}, u32[]{:S(2)}, u32[]{:S(2)}) %collective-permute-start.1) | collective-permute-done | bytes 2097184 | tf_op jit(solution)/shard_map/while/body/eval_jaxpr/ppermute | solution.py:64
  513.9 61.9 %conditional.2 = ((f32[16,4,7,128]{3,2,1,0:T(8,128)S(1)}, f32[16,4,7,128]{3,2,1,0:T(8,128)S(1)}, f32[16,4,7,128,128]{4,3,2,1,0:T(8,128)})) conditional(s32[]{:T(128)} %convert_element_type.80, (f32[16,4,7,128]{3,2,1,0:T(8,128)S(1)}, f32[16,4,7,128]{3,2,1,0:T(8,128)S(1)}, f32[16,4,7,128,128]{4,3,2,1,0:T(8,128)}) %tuple.55, ...), branch_computations={%region_4.4_spmd, %region_5.7_spmd} | conditional | flops 3824271360 | bytes 169345056 | solution.py:66
  513.9 15.0 %bitcast_reduce_fusion = (f32[16,4,7,128]{3,2,1,0:T(8,128)S(1)}, f32[16,4,128,128,7]{3,2,4,1,0:T(8,128)}) fusion(bf16[16,128,4,7,128]{4,1,3,2,0:T(8,128)(2,1)} %get-tuple-element.229, bf16[16,128,4,128]{3,1,2,0:T(8,128)(2,1)S(1)} %get-tuple-element.228), kind=kOutput, calls=%fused_computation.1 | convolution fusion | flops 1893670912 | bytes 46366720 | tf_op jit(solution)/shard_map/while/body/eval_jaxpr/cond/branch_1_fun/bqkgd,bskd->bkgqs/dot_general | solution.py:27
  528.9 13.0 %fusion.3 = f32[16,4,7,128]{3,2,1,0:T(8,128)S(1)} fusion(f32[16,4,128,128,7]{3,2,4,1,0:T(8,128)} %get-tuple-element.284, f32[16,4,7,128]{3,2,1,0:T(8,128)S(1)} %max.2), kind=kLoop, calls=%fused_computation.5 | loop fusion | flops 21962752 | bytes 29818880 | tf_op jit(solution)/shard_map/while/body/eval_jaxpr/cond/branch_1_fun/reduce_sum | solution.py:33
  541.9 0.2 multiply_add_fusion.1
  542.1 33.7 %multiply_add_fusion = f32[16,4,7,128,128]{4,3,2,1,0:T(8,128)} fusion(f32[16,4,7,128,128]{4,3,2,1,0:T(8,128)} %get-tuple-element.231, f32[16,4,7,128]{3,2,1,0:T(8,128)S(1)} %get-tuple-element.282, f32[16,4,128,128,7]{3,2,4,1,0:T(8,128)} %get-tuple-element.284, f32[16,4,7,128]{3,2,1,0:T(8,128)S(1)} %max.2, bf16[16,128,4,128]{3,1,2,0:T(8,128)(2,1)} %get-tuple-element.232), kind=kOutput, calls=%fused_computation.3 | convolution fusion | flops 1908408320 | bytes 90636288 | tf_op jit(solution)/shard_map/while/body/eval_jaxpr/cond/branch_1_fun/bkgqs,bskd->bkgqd/dot_general | solution.py:34
  575.8 1.3 copy.75
  577.1 3.2 copy.76
  580.3 71.3 %fusion.15 = bf16[16,128,3584]{2,1,0:T(8,128)(2,1)} fusion(bf16[16,128,3584]{2,1,0:T(8,128)(2,1)} %param.11, bf16[4,7,128,3584,1]{3,2,1,0,4:T(8,128)(2,1)} %bitcast.83, f32[16,4,7,128,128]{4,3,2,1,0:T(8,128)} %get-tuple-element.247, f32[16,4,7,128]{3,2,1,0:T(8,128)S(1)} %get-tuple-element.248), kind=kOutput, calls=%fused_computation.20 | convolution fusion | flops 52650049536 | bytes 84639744 | tf_op jit(solution)/shard_map/bkgqd,kgde->bqe/dot_general | solution.py:72
  (11 shorter events, 0.2 us)
Async XLA Ops:
  0.0 8.1 %copy-start.1 = (bf16[3584]{0:T(1024)(128)(2,1)S(1)}, bf16[3584]{0:T(1024)(128)(2,1)}, u32[]{:S(2)}) copy-start(bf16[3584]{0:T(1024)(128)(2,1)} %param.13) | copy-start | bytes 21508
  21.8 11.4 %copy-start.2 = (s32[16,128]{1,0:T(8,128)S(1)}, s32[16,128]{1,0:T(8,128)}, u32[]{:S(2)}) copy-start(s32[16,128]{1,0:T(8,128)} %param.12) | copy-start | bytes 24580
  187.2 13.5 %copy-start.3 = (bf16[3584,512]{1,0:T(8,128)(2,1)S(1)}, bf16[3584,512]{1,0:T(8,128)(2,1)}, u32[]{:S(2)}) copy-start(bf16[3584,512]{1,0:T(8,128)(2,1)} %param.16) | copy-start | bytes 11010052
  215.8 27.2 %copy-start = (bf16[16,128,512]{2,1,0:T(8,128)(2,1)S(1)}, bf16[16,128,512]{2,1,0:T(8,128)(2,1)}, u32[]{:S(2)}) copy-start(bf16[16,128,512]{2,1,0:T(8,128)(2,1)} %fusion.37) | copy-start | bytes 6291460
  244.9 23.0 %collective-permute-start = (bf16[16,128,4,128]{3,1,2,0:T(8,128)(2,1)}, bf16[16,128,4,128]{3,1,2,0:T(8,128)(2,1)S(1)}, u32[]{:S(2)}, u32[]{:S(2)}) collective-permute-start(bf16[16,128,4,128]{3,1,2,0:T(8,128)(2,1)} %get-tuple-element.371), channel_id=1, source_target_pairs={{0,1},{1,2},{2,3},{3,0},{4,5},{5,6},{6,7},{7,4}} | collective-permute-start | bytes 6291464 | tf_op jit(solution)/shard_map/while/body/eval_jaxpr/ppermute | solution.py:64
  244.9 45.4 %collective-permute-start.1 = (bf16[16,128,4,128]{3,1,2,0:T(8,128)(2,1)}, bf16[16,128,4,128]{3,1,2,0:T(8,128)(2,1)}, u32[]{:S(2)}, u32[]{:S(2)}) collective-permute-start(bf16[16,128,4,128]{3,1,2,0:T(8,128)(2,1)} %get-tuple-element.372), channel_id=1, source_target_pairs={{0,1},{1,2},{2,3},{3,0},{4,5},{5,6},{6,7},{7,4}} | collective-permute-start | bytes 6291464 | tf_op jit(solution)/shard_map/while/body/eval_jaxpr/ppermute | solution.py:64
  356.7 23.0 %collective-permute-start = (bf16[16,128,4,128]{3,1,2,0:T(8,128)(2,1)}, bf16[16,128,4,128]{3,1,2,0:T(8,128)(2,1)S(1)}, u32[]{:S(2)}, u32[]{:S(2)}) collective-permute-start(bf16[16,128,4,128]{3,1,2,0:T(8,128)(2,1)} %get-tuple-element.371), channel_id=1, source_target_pairs={{0,1},{1,2},{2,3},{3,0},{4,5},{5,6},{6,7},{7,4}} | collective-permute-start | bytes 6291464 | tf_op jit(solution)/shard_map/while/body/eval_jaxpr/ppermute | solution.py:64
  356.7 45.4 %collective-permute-start.1 = (bf16[16,128,4,128]{3,1,2,0:T(8,128)(2,1)}, bf16[16,128,4,128]{3,1,2,0:T(8,128)(2,1)}, u32[]{:S(2)}, u32[]{:S(2)}) collective-permute-start(bf16[16,128,4,128]{3,1,2,0:T(8,128)(2,1)} %get-tuple-element.372), channel_id=1, source_target_pairs={{0,1},{1,2},{2,3},{3,0},{4,5},{5,6},{6,7},{7,4}} | collective-permute-start | bytes 6291464 | tf_op jit(solution)/shard_map/while/body/eval_jaxpr/ppermute | solution.py:64
  468.5 23.0 %collective-permute-start = (bf16[16,128,4,128]{3,1,2,0:T(8,128)(2,1)}, bf16[16,128,4,128]{3,1,2,0:T(8,128)(2,1)S(1)}, u32[]{:S(2)}, u32[]{:S(2)}) collective-permute-start(bf16[16,128,4,128]{3,1,2,0:T(8,128)(2,1)} %get-tuple-element.371), channel_id=1, source_target_pairs={{0,1},{1,2},{2,3},{3,0},{4,5},{5,6},{6,7},{7,4}} | collective-permute-start | bytes 6291464 | tf_op jit(solution)/shard_map/while/body/eval_jaxpr/ppermute | solution.py:64
  468.5 45.4 %collective-permute-start.1 = (bf16[16,128,4,128]{3,1,2,0:T(8,128)(2,1)}, bf16[16,128,4,128]{3,1,2,0:T(8,128)(2,1)}, u32[]{:S(2)}, u32[]{:S(2)}) collective-permute-start(bf16[16,128,4,128]{3,1,2,0:T(8,128)(2,1)} %get-tuple-element.372), channel_id=1, source_target_pairs={{0,1},{1,2},{2,3},{3,0},{4,5},{5,6},{6,7},{7,4}} | collective-permute-start | bytes 6291464 | tf_op jit(solution)/shard_map/while/body/eval_jaxpr/ppermute | solution.py:64
where the time goes:
time: 657 us; the launch traced here: 652 us
  matrix products  354 us (54%)
  waiting for transfers between devices  134 us (20%)
  other arithmetic  104 us (16%)
  local copies, waits for them, and re-layouts  57.6 us (9%)
    ppermute x6, waiting for transfers between devices, step_fn(): k_blk, v_blk = lax.ppermute((k_blk, v_blk), 'cp', shift_pairs)  134 us
    dot_general x4, matrix products, attend_block(): jnp.einsum('bkgqs,bskd->bkgqd', prob_blk, v_blk, preferred_element_type=j...  128 us
    dot_general x1, matrix products, local_block(): jnp.einsum('bkgqd,kgde->bqe', attn_out, w_out.reshape(n_kv, n_groups, hea...  71.3 us
    dot_general x1, matrix products, local_block(): jnp.einsum('bsd,de->bse', normed, w_query, preferred_element_type=jnp.flo...  67.9 us
    dot_general x4, matrix products, attend_block(): jnp.einsum('bqkgd,bskd->bkgqs', q_grp, k_blk, preferred_element_type=jnp....  60.4 us
    reduce_sum x4, other arithmetic, attend_block(): new_sum = run_sum * rescale + jnp.sum(prob_blk, axis=-1)  52.3 us
    another operation x2, local copies, waits for them, and re-layouts  27.6 us
    concatenate x2, other arithmetic, rotary(): jnp.concatenate([first_half * cos_part - second_half * sin_part, second_h...  22 us
  transfers between devices with their start and end apart: 6, of which 6 were waited for; matrix products, arithmetic and copies ran while one was open for 0% of the time, Pallas kernels for 0%

commit v1 on v0

v1 whole, which is shorter than its diff:
```python
import functools

import jax
import jax.numpy as jnp
from jax import lax
from jax.experimental import pallas as pl
from jax.experimental.pallas import tpu as pltpu
from jax.sharding import PartitionSpec as P

BF = jnp.bfloat16
F32 = jnp.float32
HD = 128
VMEM_LIMIT = 60 * 1024 * 1024


def rope_tile(acc, cos, sin):
    return acc * cos + pltpu.roll(acc, HD // 2, 1) * sin


def kv_kernel(n_kv, x_ref, g_ref, wk_ref, wv_ref, cos_ref, sin_ref, kv_ref, h_ref):
    nb, seq, dim = x_ref.shape
    x = x_ref[...].reshape(nb * seq, dim).astype(F32)
    inv = lax.rsqrt(jnp.mean(x * x, axis=-1, keepdims=True) + 1e-5)
    h = (x * inv * g_ref[...].astype(F32)).astype(BF)
    h_ref[...] = h
    cos, sin = cos_ref[...], sin_ref[...]
    k = jnp.dot(h, wk_ref[...], preferred_element_type=F32)
    for n in range(n_kv):
        kv_ref[:, n, :, :] = rope_tile(k[:, n * HD:(n + 1) * HD], cos, sin).astype(BF).reshape(nb, seq, HD)
    v = jnp.dot(h, wv_ref[...], preferred_element_type=F32).astype(BF)
    for n in range(n_kv):
        kv_ref[:, n_kv + n, :, :] = v[:, n * HD:(n + 1) * HD].reshape(nb, seq, HD)


def kv_proj(x, g, wk, wv, cos, sin, b0, nbatch, nb=2):
    _, seq, dim = x.shape
    kvw = wk.shape[1]
    n_kv = kvw // HD
    rows = nb * seq
    o = b0 // nb
    return pl.pallas_call(
        functools.partial(kv_kernel, n_kv), grid=(nbatch // nb,),
        in_specs=[
            pl.BlockSpec((nb, seq, dim), lambda i: (i + o, 0, 0)),
            pl.BlockSpec((1, dim), lambda i: (0, 0)),
            pl.BlockSpec((dim, kvw), lambda i: (0, 0)),
            pl.BlockSpec((dim, kvw), lambda i: (0, 0)),
            pl.BlockSpec((rows, HD), lambda i: (i + o, 0)),
            pl.BlockSpec((rows, HD), lambda i: (i + o, 0)),
        ],
        out_specs=[
            pl.BlockSpec((nb, 2 * n_kv, seq, HD), lambda i: (i, 0, 0, 0)),
            pl.BlockSpec((rows, dim), lambda i: (i, 0)),
        ],
        out_shape=[
            jax.ShapeDtypeStruct((nbatch, 2 * n_kv, seq, HD), BF),
            jax.ShapeDtypeStruct((nbatch * seq, dim), BF),
        ],
        compiler_params=pltpu.CompilerParams(vmem_limit_bytes=VMEM_LIMIT),
        cost_estimate=pl.CostEstimate(flops=4 * nbatch * seq * dim * kvw, bytes_accessed=4 * nbatch * seq * dim, transcendentals=0),
        name="kv_proj",
    )(x, g, wk, wv, cos, sin)


def q_kernel(mc, ha_ref, hb_ref, w_ref, cos_ref, sin_ref, q_ref):
    n_heads = w_ref.shape[1] // HD
    nb = mc // HD
    for half, h_ref in enumerate((ha_ref, hb_ref)):
        base = half * ha_ref.shape[0]

        def body(i):
            r = pl.multiple_of(i * mc, mc)
            acc = jnp.dot(h_ref[pl.ds(r, mc), :], w_ref[...], preferred_element_type=F32)
            rr = pl.multiple_of(base + i * mc, mc)
            cos, sin = cos_ref[pl.ds(rr, mc), :], sin_ref[pl.ds(rr, mc), :]
            for n in range(n_heads):
                t = rope_tile(acc[:, n * HD:(n + 1) * HD], cos, sin).astype(BF)
                q_ref[pl.ds(base // HD + i * nb, nb), n, :, :] = t.reshape(nb, HD, HD)

        pl.loop(0, h_ref.shape[0] // mc)(body)


def q_proj(ha, hb, w, cos, sin, tn=512, mc=1024):
    rows = ha.shape[0] + hb.shape[0]
    dim, width = w.shape
    batch = rows // HD
    return pl.pallas_call(
        functools.partial(q_kernel, mc), grid=(width // tn,),
        in_specs=[
            pl.BlockSpec(ha.shape, lambda j: (0, 0)),
            pl.BlockSpec(hb.shape, lambda j: (0, 0)),
            pl.BlockSpec((dim, tn), lambda j: (0, j)),
            pl.BlockSpec((rows, HD), lambda j: (0, 0)),
            pl.BlockSpec((rows, HD), lambda j: (0, 0)),
        ],
        out_specs=pl.BlockSpec((batch, tn // HD, HD, HD), lambda j: (0, j, 0, 0)),
        out_shape=jax.ShapeDtypeStruct((batch, width // HD, HD, HD), BF),
        compiler_params=pltpu.CompilerParams(vmem_limit_bytes=VMEM_LIMIT),
        cost_estimate=pl.CostEstimate(flops=2 * rows * dim * width, bytes_accessed=4 * rows * dim, transcendentals=0),
        name="q_proj",
    )(ha, hb, w, cos, sin)


SCALE = 1.4426950408889634 * HD ** -0.5


def attend_heads(n_blocks, n_kv, groups, q_ref, kv_refs, o_ref):
    row = lax.broadcasted_iota(jnp.int32, (HD, HD), 0)
    col = lax.broadcasted_iota(jnp.int32, (HD, HD), 1)
    bias = jnp.where(row >= col, 0.0, -jnp.inf).astype(F32)
    for u in range(n_kv):
        k = jnp.concatenate([r[0, u] for r in kv_refs[:n_blocks]], 0)
        v = jnp.concatenate([r[0, n_kv + u] for r in kv_refs[:n_blocks]], 0).astype(F32)
        q = q_ref[0, u * groups:(u + 1) * groups].reshape(groups * HD, HD)
        scores = lax.dot_general(q, k, (((1,), (1,)), ((), ())), preferred_element_type=F32)
        for n in range(groups):
            s = scores[n * HD:(n + 1) * HD]
            s_diag = s[:, :HD] + bias
            s = s_diag if n_blocks == 1 else jnp.concatenate([s_diag, s[:, HD:]], 1)
            m = jnp.max(s, axis=-1, keepdims=True)
            p = jnp.exp2(s * SCALE - m * SCALE)
            total = jnp.sum(p, axis=-1, keepdims=True)
            acc = jnp.dot(p, v, preferred_element_type=F32)
            head = u * groups + n
            o_ref[0, :, head * HD:(head + 1) * HD] = (acc / total).astype(BF)


def attn_kernel(n_kv, groups, n_cp, q_ref, own_ref, r1_ref, r2_ref, r3_ref, o_ref):
    me = lax.axis_index("cp")
    plans = ((own_ref,), (own_ref, r2_ref), (own_ref, r1_ref, r3_ref), (own_ref, r1_ref, r2_ref, r3_ref))
    for c in range(n_cp):
        @pl.when(me == c)
        def _(c=c):
            attend_heads(c + 1, n_kv, groups, q_ref, plans[c], o_ref)


def attention(q, own, r1, r2, r3, b0, n_cp):
    batch, n2, seq, hd = own.shape
    heads = q.shape[1]
    n_kv = n2 // 2
    kv_spec = pl.BlockSpec((1, n2, seq, hd), lambda b: (b, 0, 0, 0))
    return pl.pallas_call(
        functools.partial(attn_kernel, n_kv, heads // n_kv, n_cp), grid=(batch,),
        in_specs=[pl.BlockSpec((1, heads, seq, hd), lambda b: (b + b0, 0, 0, 0)), kv_spec, kv_spec, kv_spec, kv_spec],
        out_specs=pl.BlockSpec((1, seq, heads * hd), lambda b: (b, 0, 0)),
        out_shape=jax.ShapeDtypeStruct((batch, seq, heads * hd), BF),
        compiler_params=pltpu.CompilerParams(vmem_limit_bytes=VMEM_LIMIT),
        cost_estimate=pl.CostEstimate(flops=16 * batch * heads * seq * seq * hd * 2, bytes_accessed=4 * batch * heads * seq * hd, transcendentals=0),
        name="attention",
    )(q, own, r1, r2, r3)


def out_kernel(mc, aliased, o_ref, w_ref, x_ref, *rest):
    y_ref = rest[-1]
    tn = w_ref.shape[1]
    nb = mc // HD

    def body(i):
        r = pl.multiple_of(i * mc, mc)
        acc = jnp.dot(o_ref[pl.ds(r, mc), :], w_ref[...], preferred_element_type=F32)
        b = pl.ds(i * nb, nb)
        y_ref[b] = (x_ref[b].astype(F32) + acc.reshape(nb, HD, tn)).astype(BF)

    pl.loop(0, o_ref.shape[0] // mc)(body)


def out_proj(o, w, x, b0, y_prev=None, tn=512, mc=1024):
    rows, dim = o.shape
    width = w.shape[1]
    batch = rows // HD
    spec = pl.BlockSpec((batch, HD, tn), lambda j: (b0 // batch, 0, j))
    args = [o, w, x]
    in_specs = [pl.BlockSpec((rows, dim), lambda j: (0, 0)), pl.BlockSpec((dim, tn), lambda j: (0, j)), spec]
    if y_prev is not None:
        args.append(y_prev)
        in_specs.append(pl.BlockSpec(memory_space=pl.ANY))
    return pl.pallas_call(
        functools.partial(out_kernel, mc, y_prev is not None), grid=(width // tn,),
        in_specs=in_specs, out_specs=spec,
        out_shape=jax.ShapeDtypeStruct(x.shape, BF),
        input_output_aliases={} if y_prev is None else {3: 0},
        compiler_params=pltpu.CompilerParams(vmem_limit_bytes=VMEM_LIMIT),
        cost_estimate=pl.CostEstimate(flops=2 * rows * dim * width, bytes_accessed=4 * rows * dim, transcendentals=0),
        name="out_proj",
    )(*args)


def rope_tables(positions):
    half = HD // 2
    inv_freq = 10000.0 ** (-2.0 * jnp.arange(half, dtype=F32) / HD)
    angles = positions.reshape(-1, 1).astype(F32) * inv_freq
    cos, sin = jnp.cos(angles), jnp.sin(angles)
    return jnp.concatenate([cos, cos], 1), jnp.concatenate([-sin, sin], 1)


def solution(mesh):
    n_cp = mesh.shape['cp']

    def local_block(hidden, positions, norm_gain, w_query, w_key, w_value, w_out):
        batch, seq, dim = hidden.shape
        heads = w_out.shape[0]
        half = batch // 2
        gain = norm_gain.reshape(1, dim)
        cos, sin = rope_tables(positions)
        own, h = [], []
        for i in range(2):
            kv_i, h_i = kv_proj(hidden, gain, w_key, w_value, cos, sin, i * half, half)
            own.append(kv_i)
            h.append(h_i)
        r1 = [lax.ppermute(t, 'cp', [(0, 2), (1, 3)]) for t in own]
        r2 = [lax.ppermute(t, 'cp', [(0, 1), (2, 3)]) for t in own]
        r3 = [lax.ppermute(t, 'cp', [(2, 3), (3, 2)]) for t in r1]
        q = q_proj(h[0], h[1], w_query, cos, sin)
        y = None
        w_flat = w_out.reshape(heads * HD, dim)
        for i in range(2):
            o = attention(q, own[i], r1[i], r2[i], r3[i], i * half, n_cp)
            y = out_proj(o.reshape(half * seq, heads * HD), w_flat, hidden, i * half, y)
        return y

    act_spec = P('dp', 'cp', None)
    return jax.shard_map(local_block, mesh=mesh, in_specs=(act_spec, P('dp', 'cp'), P(), P(), P(), P(), P()), out_specs=act_spec, check_vma=False)
```

time: 657 us -> 255 us (0.39)
  matrix products: 354 us -> 0 us
  Pallas kernels: 0 us -> 207 us
  waiting for transfers between devices: 134 us -> 28.5 us
  other arithmetic: 104 us -> 6.33 us
  local copies, waits for them, and re-layouts: 57.6 us -> 1.31 us
  starting transfers between devices: 2.44 us -> 11.7 us
    dot_general x12 -> x0, matrix products: 354 us -> none  [the longest x4 128 us: attend_block(): jnp.einsum('bkgqs,bskd->bkgqd', prob_blk, v_blk, preferred_element_type=j...]
    pallas_call x0 -> x7, Pallas kernels: none -> 207 us  [the longest x2 66.5 us: out_proj(): pl.pallas_call(functools.partial(out_kernel, mc, y_prev is not None), gri...]
    ppermute x6, waiting for transfers between devices: 134 us -> 28.5 us  [the longest x2 28.5 us: local_block(): r1 = [lax.ppermute(t, 'cp', [(0, 2), (1, 3)]) for t in own]]
    reduce_sum x5 -> x0, other arithmetic: 60.4 us -> none  [the longest x4 52.3 us: attend_block(): new_sum = run_sum * rescale + jnp.sum(prob_blk, axis=-1)]
    another operation x2 -> x0, local copies, waits for them, and re-layouts: 27.6 us -> none
    concatenate x2 -> x1, other arithmetic: 22 us -> 1.9 us  [rope_tables(): return (jnp.concatenate([cos, cos], 1), jnp.concatenate([-sin, sin], 1))]
    another operation x3 -> x0, other arithmetic: 16.8 us -> none
    while x7 -> x0, local copies, waits for them, and re-layouts: 15.3 us -> none
  transfers between devices with their start and end apart: 6 -> 6, of which waited for: 6 -> 1; matrix products, arithmetic and copies ran while one was open for 0% -> 0% of each run, Pallas kernels for 0% -> 53%
where the time goes in v1:
time: 255 us
  Pallas kernels  207 us (81%)
  waiting for transfers between devices  28.5 us (11%)
  starting transfers between devices  11.7 us (5%)
  other arithmetic  6.33 us (2%)
    pallas_call x2, Pallas kernels, out_proj(): pl.pallas_call(functools.partial(out_kernel, mc, y_prev is not None), gri...  66.5 us
    pallas_call x1, Pallas kernels, q_proj(): pl.pallas_call(functools.partial(q_kernel, mc), grid=(width // tn,), in_s...  64.9 us
    pallas_call x2, Pallas kernels, attention(): pl.pallas_call(functools.partial(attn_kernel, n_kv, heads // n_kv, n_cp),...  45.7 us
    pallas_call x2, Pallas kernels, kv_proj(): pl.pallas_call(functools.partial(kv_kernel, n_kv), grid=(nbatch // nb,),...  29.6 us
    ppermute x2, waiting for transfers between devices, local_block(): r1 = [lax.ppermute(t, 'cp', [(0, 2), (1, 3)]) for t in own]  28.5 us
    ppermute x2, starting transfers between devices, local_block(): r3 = [lax.ppermute(t, 'cp', [(2, 3), (3, 2)]) for t in r1]  6.57 us
  transfers between devices with their start and end apart: 6, of which 1 were waited for; matrix products, arithmetic and copies ran while one was open for 0% of the time, Pallas kernels for 53%

profile of v1, /device:TPU:3, one launch (start us, length us, event | category | flops | bytes accessed | tf_op | source)
XLA Modules:
  0.0 254.7 jit_solution(18179191840625558155)
XLA Ops:
  0.0 1.3 reshape.26.g_ref
  1.3 0.7 convert_bitcast_fusion
  2.0 3.7 %fusion = (f32[2048,64]{1,0:T(8,128)S(1)}, f32[2048,64]{1,0:T(8,128)S(1)}, f32[2048,64]{1,0:T(8,128)S(1)}) fusion(f32[64]{0:T(128)S(1)} %multiply_power_fusion, f32[2048]{0:T(1024)S(1)} %convert_bitcast_fusion), kind=kLoop, calls=%fused_computation.4 | loop fusion | flops 262144 | bytes 1581312 | tf_op jit(solution)/shard_map/neg | solution.py:193
  5.7 1.9 pad_maximum_fusion
  7.6 14.8 %kv_proj.2 = (bf16[8,8,128,128]{3,2,1,0:T(8,128)(2,1)}, bf16[1024,3584]{1,0:T(8,128)(2,1)}) custom-call(bf16[16,128,3584]{2,1,0:T(8,128)(2,1)} %x_ref.7, bf16[1,3584]{1,0:T(2,128)(2,1)} %reshape.26.g_ref, bf16[3584,512]{1,0:T(8,128)(2,1)} %wk_ref.3, bf16[3584,512]{1,0:T(8,128)(2,1)} %wv_ref.3, f32[2048,128]{1,0:T(8,128)} %get-tuple-element.16.cos_ref, ...), custom_call_target="tpu_custom_call" | custom-call | flops 7516192768 | bytes 14680064 | tf_op jit(solution)/shard_map/kv_proj/pallas_call | solution.py:41
  22.4 1.3 collective-permute-start.3
  23.7 14.9 %kv_proj.3 = (bf16[8,8,128,128]{3,2,1,0:T(8,128)(2,1)}, bf16[1024,3584]{1,0:T(8,128)(2,1)}) custom-call(bf16[16,128,3584]{2,1,0:T(8,128)(2,1)} %x_ref.7, bf16[1,3584]{1,0:T(2,128)(2,1)} %reshape.26.g_ref, bf16[3584,512]{1,0:T(8,128)(2,1)} %wk_ref.3, bf16[3584,512]{1,0:T(8,128)(2,1)} %wv_ref.3, f32[2048,128]{1,0:T(8,128)} %get-tuple-element.16.cos_ref, ...), custom_call_target="tpu_custom_call" | custom-call | flops 7516192768 | bytes 14680064 | tf_op jit(solution)/shard_map/kv_proj/pallas_call | solution.py:41
  38.6 1.3 collective-permute-start
  39.9 1.3 collective-permute-start.1
  41.2 1.3 collective-permute-start.4
  42.5 28.5 %collective-permute-done.3.r1_ref = bf16[8,8,128,128]{3,2,1,0:T(8,128)(2,1)} collective-permute-done((bf16[8,8,128,128]{3,2,1,0:T(8,128)(2,1)}, bf16[8,8,128,128]{3,2,1,0:T(8,128)(2,1)}, u32[]{:S(2)}, u32[]{:S(2)}) %collective-permute-start.3) | collective-permute-done | bytes 2097184 | tf_op jit(solution)/shard_map/ppermute | solution.py:210
  70.9 4.6 %collective-permute-start.5 = (bf16[8,8,128,128]{3,2,1,0:T(8,128)(2,1)}, bf16[8,8,128,128]{3,2,1,0:T(8,128)(2,1)}, u32[]{:S(2)}, u32[]{:S(2)}) collective-permute-start(bf16[8,8,128,128]{3,2,1,0:T(8,128)(2,1)} %collective-permute-done.3.r1_ref), channel_id=1, source_target_pairs={{2,3},{3,2},{6,7},{7,6}} | collective-permute-start | bytes 6291464 | tf_op jit(solution)/shard_map/ppermute | solution.py:212
  75.6 64.9 %q_proj.1.q_ref = bf16[16,28,128,128]{3,2,1,0:T(8,128)(2,1)} custom-call(bf16[1024,3584]{1,0:T(8,128)(2,1)} %get-tuple-element.9.ha_ref, bf16[1024,3584]{1,0:T(8,128)(2,1)} %get-tuple-element.10.hb_ref, bf16[3584,3584]{1,0:T(8,128)(2,1)} %w_ref.1, f32[2048,128]{1,0:T(8,128)} %get-tuple-element.16.cos_ref, f32[2048,128]{1,0:T(8,128)} %get-tuple-element.17.sin_ref), custom_call_target="tpu_custom_call" | custom-call | flops 52613349376 | bytes 29360128 | tf_op jit(solution)/shard_map/q_proj/pallas_call | solution.py:87
  140.5 0.0 collective-permute-done.r1_ref
  140.5 0.0 copy-start
  140.5 1.9 collective-permute-start.2
  142.4 0.0 collective-permute-done.4.r2_ref
  142.5 0.0 collective-permute-done.5.r3_ref
  142.5 22.7 %attention.3 = bf16[8,128,3584]{2,1,0:T(8,128)(2,1)} custom-call(bf16[16,28,128,128]{3,2,1,0:T(8,128)(2,1)} %q_proj.1.q_ref, bf16[8,8,128,128]{3,2,1,0:T(8,128)(2,1)} %get-tuple-element.12.own_ref, bf16[8,8,128,128]{3,2,1,0:T(8,128)(2,1)} %collective-permute-done.3.r1_ref, bf16[8,8,128,128]{3,2,1,0:T(8,128)(2,1)} %collective-permute-done.4.r2_ref, ...), custom_call_target="tpu_custom_call" | custom-call | flops 15032385536 | bytes 14680064 | tf_op jit(solution)/shard_map/attention/pallas_call | solution.py:142
  165.2 0.0 copy-done
  165.2 33.3 %out_proj.2.rest_0_ = bf16[16,128,3584]{2,1,0:T(8,128)(2,1)} custom-call(bf16[1024,3584]{1,0:T(8,128)(2,1)} %bitcast.8, bf16[3584,3584]{1,0:T(8,128)(2,1)} %bitcast.5, bf16[16,128,3584]{2,1,0:T(8,128)(2,1)} %x_ref.7), custom_call_target="tpu_custom_call" | custom-call | flops 26306674688 | bytes 14680064 | tf_op jit(solution)/shard_map/out_proj/pallas_call | solution.py:177
  198.4 0.0 collective-permute-done.1.r2_ref
  198.4 0.0 collective-permute-done.2.r3_ref
  198.5 23.0 %attention.2 = bf16[8,128,3584]{2,1,0:T(8,128)(2,1)} custom-call(bf16[16,28,128,128]{3,2,1,0:T(8,128)(2,1)} %q_proj.1.q_ref, bf16[8,8,128,128]{3,2,1,0:T(8,128)(2,1)} %get-tuple-element.11.own_ref, bf16[8,8,128,128]{3,2,1,0:T(8,128)(2,1)} %copy-done, bf16[8,8,128,128]{3,2,1,0:T(8,128)(2,1)} %collective-permute-done.1.r2_ref, ...), custom_call_target="tpu_custom_call" | custom-call | flops 15032385536 | bytes 14680064 | tf_op jit(solution)/shard_map/attention/pallas_call | solution.py:142
  221.4 33.3 %out_proj.3 = bf16[16,128,3584]{2,1,0:T(8,128)(2,1)} custom-call(bf16[1024,3584]{1,0:T(8,128)(2,1)} %bitcast.7, bf16[3584,3584]{1,0:T(8,128)(2,1)} %bitcast.6, bf16[16,128,3584]{2,1,0:T(8,128)(2,1)} %x_ref.7, bf16[16,128,3584]{2,1,0:T(8,128)(2,1)} %out_proj.2.rest_0_), custom_call_target="tpu_custom_call", output_to_operand_aliasing={{}: (3, {})} | custom-call | flops 26306674688 | bytes 14680064 | tf_op jit(solution)/shard_map/out_proj/pallas_call | solution.py:177
  (1 shorter events, 0.0 us)
Async XLA Ops:
  22.4 48.5 %collective-permute-start.3 = (bf16[8,8,128,128]{3,2,1,0:T(8,128)(2,1)}, bf16[8,8,128,128]{3,2,1,0:T(8,128)(2,1)}, u32[]{:S(2)}, u32[]{:S(2)}) collective-permute-start(bf16[8,8,128,128]{3,2,1,0:T(8,128)(2,1)} %get-tuple-element.12.own_ref), channel_id=1, source_target_pairs={{0,2},{1,3},{4,6},{5,7}} | collective-permute-start | bytes 6291464 | tf_op jit(solution)/shard_map/ppermute | solution.py:210
  38.6 101.9 %collective-permute-start = (bf16[8,8,128,128]{3,2,1,0:T(8,128)(2,1)}, bf16[8,8,128,128]{3,2,1,0:T(8,128)(2,1)S(1)}, u32[]{:S(2)}, u32[]{:S(2)}) collective-permute-start(bf16[8,8,128,128]{3,2,1,0:T(8,128)(2,1)} %get-tuple-element.11.own_ref), channel_id=1, source_target_pairs={{0,2},{1,3},{4,6},{5,7}} | collective-permute-start | bytes 6291464 | tf_op jit(solution)/shard_map/ppermute | solution.py:210
  39.9 158.6 %collective-permute-start.1 = (bf16[8,8,128,128]{3,2,1,0:T(8,128)(2,1)}, bf16[8,8,128,128]{3,2,1,0:T(8,128)(2,1)}, u32[]{:S(2)}, u32[]{:S(2)}) collective-permute-start(bf16[8,8,128,128]{3,2,1,0:T(8,128)(2,1)} %get-tuple-element.11.own_ref), channel_id=1, source_target_pairs={{0,1},{2,3},{4,5},{6,7}} | collective-permute-start | bytes 6291464 | tf_op jit(solution)/shard_map/ppermute | solution.py:211
  41.2 101.3 %collective-permute-start.4 = (bf16[8,8,128,128]{3,2,1,0:T(8,128)(2,1)}, bf16[8,8,128,128]{3,2,1,0:T(8,128)(2,1)}, u32[]{:S(2)}, u32[]{:S(2)}) collective-permute-start(bf16[8,8,128,128]{3,2,1,0:T(8,128)(2,1)} %get-tuple-element.12.own_ref), channel_id=1, source_target_pairs={{0,1},{2,3},{4,5},{6,7}} | collective-permute-start | bytes 6291464 | tf_op jit(solution)/shard_map/ppermute | solution.py:211
  70.9 71.5 %collective-permute-start.5 = (bf16[8,8,128,128]{3,2,1,0:T(8,128)(2,1)}, bf16[8,8,128,128]{3,2,1,0:T(8,128)(2,1)}, u32[]{:S(2)}, u32[]{:S(2)}) collective-permute-start(bf16[8,8,128,128]{3,2,1,0:T(8,128)(2,1)} %collective-permute-done.3.r1_ref), channel_id=1, source_target_pairs={{2,3},{3,2},{6,7},{7,6}} | collective-permute-start | bytes 6291464 | tf_op jit(solution)/shard_map/ppermute | solution.py:212
  140.5 24.7 %copy-start = (bf16[8,8,128,128]{3,2,1,0:T(8,128)(2,1)}, bf16[8,8,128,128]{3,2,1,0:T(8,128)(2,1)S(1)}, u32[]{:S(2)}) copy-start(bf16[8,8,128,128]{3,2,1,0:T(8,128)(2,1)S(1)} %collective-permute-done.r1_ref) | copy-start | bytes 6291460
  140.5 57.9 %collective-permute-start.2 = (bf16[8,8,128,128]{3,2,1,0:T(8,128)(2,1)S(1)}, bf16[8,8,128,128]{3,2,1,0:T(8,128)(2,1)}, u32[]{:S(2)}, u32[]{:S(2)}) collective-permute-start(bf16[8,8,128,128]{3,2,1,0:T(8,128)(2,1)S(1)} %collective-permute-done.r1_ref), channel_id=1, source_target_pairs={{2,3},{3,2},{6,7},{7,6}} | collective-permute-start | bytes 6291464 | tf_op jit(solution)/shard_map/ppermute | solution.py:212

commit v2 on v0

v2 whole, which is shorter than its diff:
```python
import functools

import jax
import jax.numpy as jnp
import numpy as np
from jax import lax
from jax.experimental import pallas as pl
from jax.experimental.pallas import tpu as pltpu
from jax.sharding import PartitionSpec as P

BF = jnp.bfloat16
F32 = jnp.float32
HD = 128
TN = 512
VMEM_LIMIT = 67043328
SCALE = 1.4426950408889634 * HD ** -0.5


def cdot(a, b):
    return jnp.dot(a, b, preferred_element_type=F32)


def rope_tile(acc, cos, sin):
    return acc * cos + pltpu.roll(acc, HD // 2, 1) * sin


def sin_cos(angle):
    n = jnp.floor(angle * 0.6366197723675814 + 0.5)
    r = angle - n * 1.5703125
    r = r - n * 4.837512969970703e-4
    r = r - n * 7.549790126404332e-08
    r2 = r * r
    s = r + r * r2 * (-1.6666654611e-1 + r2 * (8.3321608736e-3 + r2 * -1.9515295891e-4))
    c = 1.0 - 0.5 * r2 + r2 * r2 * (4.166664568298827e-2 + r2 * (-1.388731625493765e-3 + r2 * 2.443315711809948e-5))
    q = n.astype(jnp.int32)
    odd = (q & 1) == 1
    sin_v = jnp.where(odd, c, s)
    cos_v = jnp.where(odd, s, c)
    sin_v = jnp.where((q & 2) == 2, -sin_v, sin_v)
    cos_v = jnp.where(((q + 1) & 2) == 2, -cos_v, cos_v)
    return sin_v, cos_v


def attend_heads(n_blocks, n_kv, groups, q_ref, kv_refs, o_ref):
    row = lax.broadcasted_iota(jnp.int32, (HD, HD), 0)
    col = lax.broadcasted_iota(jnp.int32, (HD, HD), 1)
    bias = jnp.where(row >= col, 0.0, -jnp.inf).astype(F32)
    for u in range(n_kv):
        k = jnp.concatenate([r[u] for r in kv_refs[:n_blocks]], 0)
        v = jnp.concatenate([r[n_kv + u] for r in kv_refs[:n_blocks]], 0).astype(F32)
        q = q_ref[u * groups:(u + 1) * groups].reshape(groups * HD, HD)
        scores = lax.dot_general(q, k, (((1,), (1,)), ((), ())), preferred_element_type=F32)
        for n in range(groups):
            s = scores[n * HD:(n + 1) * HD]
            s_diag = s[:, :HD] + bias
            s = s_diag if n_blocks == 1 else jnp.concatenate([s_diag, s[:, HD:]], 1)
            m = jnp.max(s, axis=-1, keepdims=True)
            p = jnp.exp2(s * SCALE - m * SCALE)
            total = jnp.sum(p, axis=-1, keepdims=True)
            head = u * groups + n
            o_ref[:, head * HD:(head + 1) * HD] = (cdot(p, v) / total).astype(BF)


def attend_any(me, n_cp, n_kv, groups, q_ref, own, r1, r2, r3, o_ref):
    plans = ((own,), (own, r2), (own, r1, r3), (own, r1, r2, r3))
    for c in range(n_cp):
        @pl.when(me == c)
        def _(c=c):
            attend_heads(c + 1, n_kv, groups, q_ref, plans[c], o_ref)


def front_kernel(n_kv, n_first, forward_q, forward_a,
                 x_hbm, pos_ref, gain_ref, freq_ref, wq_hbm, wk_hbm, wv_hbm,
                 q_hbm, o_hbm, own_hbm, r1_hbm, r2_hbm, r3_hbm,
                 h_ref, kv_ref, cos_ref, sin_ref, x_buf, w_buf, q_buf, qa_buf, ra_buf, oa_buf,
                 x_sem, w_sem, q_sem, qa_sem, ra_sem, oa_sem, own_sem,
                 send1, recv1, send2, recv2, send3, recv3):
    batch, seq, dim = x_hbm.shape
    heads = q_hbm.shape[1]
    groups = heads // n_kv
    nb = x_buf.shape[1]
    n_chunks = batch // nb
    rows = nb * seq
    n_tiles = wq_hbm.shape[1] // TN
    tile_heads = TN // HD
    me = lax.axis_index("cp")
    low, high, odd = me < 2, me >= 2, lax.rem(me, 2) == 1

    def x_copy(i):
        s = lax.rem(i, 2)
        return pltpu.make_async_copy(x_hbm.at[pl.ds(i * nb, nb)], x_buf.at[s], x_sem.at[s])

    def wq_copy(j):
        s = lax.rem(j + 2, 3)
        return pltpu.make_async_copy(wq_hbm.at[:, pl.ds(pl.multiple_of(j * TN, TN), TN)], w_buf.at[s], w_sem.at[s])

    wk_copy = pltpu.make_async_copy(wk_hbm, w_buf.at[0], w_sem.at[0])
    wv_copy = pltpu.make_async_copy(wv_hbm, w_buf.at[1], w_sem.at[1])
    x_copy(0).start()
    wk_copy.start()
    wv_copy.start()
    x_copy(1).start()
    wq_copy(0).start()

    def part(ref, i):
        return ref.at[pl.ds(i * nb, nb)]

    def remote(src, dst, i, send, recv, target):
        return pltpu.make_async_remote_copy(
            src_ref=part(src, i), dst_ref=part(dst, i), send_sem=send.at[i], recv_sem=recv.at[i],
            device_id={"cp": target}, device_id_type=pl.DeviceIdType.MESH)

    def copy1(i):
        return remote(kv_ref, r1_hbm, i, send1, recv1, lax.rem(me + 2, 4))

    def copy2(i):
        return remote(kv_ref, r2_hbm, i, send2, recv2, me + 1 - 2 * lax.rem(me, 2))

    def copy3(i):
        return remote(r1_hbm, r3_hbm, i, send3, recv3, me + 1 - 2 * lax.rem(me, 2))

    lane = lax.broadcasted_iota(jnp.int32, (1, HD), 1)
    sign = jnp.where(lane < HD // 2, -1.0, 1.0).astype(F32)

    def table(b):
        pos = jnp.broadcast_to(pos_ref[pl.ds(b, 1), :].astype(F32), (HD, HD)).T
        s, c = sin_cos(pos * freq_ref[...])
        at = pl.ds(pl.multiple_of(b * HD, HD), HD)
        cos_ref[at, :] = c
        sin_ref[at, :] = s * sign

    pl.loop(0, batch)(table)

    barrier = pltpu.get_barrier_semaphore()
    for target in (lax.rem(me + 2, 4), me + 1 - 2 * lax.rem(me, 2)):
        pl.semaphore_signal(barrier, inc=1, device_id={"cp": target}, device_id_type=pl.DeviceIdType.MESH)
    pl.semaphore_wait(barrier, 2)

    def send(i):
        @pl.when(low)
        def _():
            copy1(i).start()

        @pl.when(jnp.logical_not(odd))
        def _():
            copy2(i).start()

    wk_copy.wait()
    wv_copy.wait()

    def kv_chunk(i):
        x_copy(i).wait()
        at = pl.ds(pl.multiple_of(i * rows, rows), rows)
        x = x_buf[lax.rem(i, 2)].reshape(rows, dim).astype(F32)
        inv = lax.rsqrt(jnp.mean(x * x, axis=-1, keepdims=True) + 1e-5)
        h = (x * inv * gain_ref[...].astype(F32)).astype(BF)
        h_ref[at, :] = h
        cos, sin = cos_ref[at, :], sin_ref[at, :]
        k = cdot(h, w_buf[0])
        to = pl.ds(i * nb, nb)
        for n in range(n_kv):
            kv_ref[to, n] = rope_tile(k[:, n * HD:(n + 1) * HD], cos, sin).astype(BF).reshape(nb, seq, HD)
        v = cdot(h, w_buf[1]).astype(BF)
        for n in range(n_kv):
            kv_ref[to, n_kv + n] = v[:, n * HD:(n + 1) * HD].reshape(nb, seq, HD)

        @pl.when(i + 2 < n_chunks)
        def _():
            x_copy(i + 2).start()

        @pl.when(i > 0)
        def _():
            send(i - 1)

    pl.loop(0, n_chunks)(kv_chunk)
    wq_copy(1).start()

    def forward(i):
        @pl.when(high)
        def _():
            copy1(i).wait_recv()
            copy3(i).start()

    def q_copy(j):
        s = lax.rem(j, 2)
        return pltpu.make_async_copy(q_buf.at[s], q_hbm.at[:, pl.ds(j * tile_heads, tile_heads)], q_sem.at[s])

    own_copy = pltpu.make_async_copy(kv_ref.at[pl.ds(n_first, batch - n_first)], own_hbm, own_sem)
    mc = 1024

    def q_tile(j):
        @pl.when(j == 0)
        def _():
            send(n_chunks - 1)
            own_copy.start()

        for at, chunk in forward_q:
            @pl.when(j == at)
            def _(chunk=chunk):
                forward(chunk)

        wq_copy(j).wait()

        @pl.when(jnp.logical_and(j > 0, j + 1 < n_tiles))
        def _():
            wq_copy(j + 1).start()

        @pl.when(j >= 2)
        def _():
            q_copy(j - 2).wait()

        ws, qs = lax.rem(j + 2, 3), lax.rem(j, 2)

        def rows_step(i):
            at = pl.ds(pl.multiple_of(i * mc, mc), mc)
            acc = cdot(h_ref[at, :], w_buf[ws])
            cos, sin = cos_ref[at, :], sin_ref[at, :]
            for n in range(tile_heads):
                t = rope_tile(acc[:, n * HD:(n + 1) * HD], cos, sin).astype(BF)
                q_buf[qs, pl.ds(i * (mc // HD), mc // HD), n] = t.reshape(mc // HD, HD, HD)

        pl.loop(0, batch * seq // mc)(rows_step)
        q_copy(j).start()

    pl.loop(0, n_tiles)(q_tile)
    q_copy(n_tiles - 2).wait()
    q_copy(n_tiles - 1).wait()

    first_chunks = n_first // nb
    for i in range(first_chunks):
        @pl.when(odd)
        def _(i=i):
            copy2(i).wait_recv()

        @pl.when(high)
        def _(i=i):
            copy3(i).wait_recv()

    def loads(b):
        s = lax.rem(b, 2)
        pairs = [(None, pltpu.make_async_copy(q_hbm.at[b], qa_buf.at[s], qa_sem.at[s]))]
        for n, (ref, used) in enumerate(((r1_hbm, high), (r2_hbm, odd), (r3_hbm, high))):
            pairs.append((used, pltpu.make_async_copy(ref.at[b], ra_buf.at[s, n], ra_sem.at[s, n])))
        return pairs

    def start_loads(b):
        for used, copy in loads(b):
            if used is None:
                copy.start()
            else:
                pl.when(used)(copy.start)

    def wait_loads(b):
        for used, copy in loads(b):
            if used is None:
                copy.wait()
            else:
                pl.when(used)(copy.wait)

    def o_copy(b):
        s = lax.rem(b, 2)
        return pltpu.make_async_copy(oa_buf.at[s], o_hbm.at[pl.ds(pl.multiple_of(b * seq, seq), seq)], oa_sem.at[s])

    start_loads(0)

    def attend(b):
        for at, chunk in forward_a:
            @pl.when(b == at)
            def _(chunk=chunk):
                forward(chunk)

        wait_loads(b)

        @pl.when(b + 1 < n_first)
        def _():
            start_loads(b + 1)

        @pl.when(b >= 2)
        def _():
            o_copy(b - 2).wait()

        s = lax.rem(b, 2)
        attend_any(me, 4, n_kv, groups, qa_buf.at[s], kv_ref.at[b], ra_buf.at[s, 0], ra_buf.at[s, 1], ra_buf.at[s, 2], oa_buf.at[s])
        o_copy(b).start()

    pl.loop(0, n_first)(attend)
    o_copy(n_first - 2).wait()
    o_copy(n_first - 1).wait()
    own_copy.wait()
    done = [c for _, c in forward_q] + [c for _, c in forward_a]
    for i in range(n_chunks):
        if i not in done:
            forward(i)
    for i in range(n_chunks):
        @pl.when(low)
        def _(i=i):
            copy1(i).wait_send()

        @pl.when(jnp.logical_not(odd))
        def _(i=i):
            copy2(i).wait_send()

        @pl.when(high)
        def _(i=i):
            copy3(i).wait_send()

        if i >= first_chunks:
            @pl.when(odd)
            def _(i=i):
                copy2(i).wait_recv()

            @pl.when(high)
            def _(i=i):
                copy3(i).wait_recv()


def back_kernel(n_kv, n_first, q_hbm, oa_hbm, own_hbm, r1_hbm, r2_hbm, r3_hbm, w_hbm, x_hbm,
                y_hbm, o_ref, w_buf, x_buf, y_buf, q_buf, kv_buf,
                o_sem, w_sem, x_sem, y_sem, q_sem, kv_sem):
    batch, seq, dim = x_hbm.shape
    half = batch - n_first
    heads = q_hbm.shape[1]
    groups = heads // n_kv
    n_tiles = dim // TN
    me = lax.axis_index("cp")
    high, odd = me >= 2, lax.rem(me, 2) == 1

    def w_copy(t):
        s = lax.rem(t, 2)
        col = pl.multiple_of(lax.rem(t, n_tiles) * TN, TN)
        return pltpu.make_async_copy(w_hbm.at[:, pl.ds(col, TN)], w_buf.at[s], w_sem.at[s])

    def x_copy(t):
        s = lax.rem(t, 2)
        col = pl.multiple_of(lax.rem(t, n_tiles) * TN, TN)
        return pltpu.make_async_copy(x_hbm.at[pl.ds(lax.div(t, n_tiles) * half, half), :, pl.ds(col, TN)], x_buf.at[s], x_sem.at[s])

    def y_copy(t):
        s = lax.rem(t, 2)
        col = pl.multiple_of(lax.rem(t, n_tiles) * TN, TN)
        return pltpu.make_async_copy(y_buf.at[s], y_hbm.at[pl.ds(lax.div(t, n_tiles) * half, half), :, pl.ds(col, TN)], y_sem.at[s])

    def loads(b):
        s = lax.rem(b, 2)
        pairs = [(None, pltpu.make_async_copy(q_hbm.at[n_first + b], q_buf.at[s], q_sem.at[s]))]
        for n, (ref, used, at) in enumerate(((own_hbm, None, b), (r1_hbm, high, n_first + b), (r2_hbm, odd, n_first + b), (r3_hbm, high, n_first + b))):
            pairs.append((used, pltpu.make_async_copy(ref.at[at], kv_buf.at[s, n], kv_sem.at[s, n])))
        return pairs

    def run_loads(b, act):
        for used, copy in loads(b):
            if used is None:
                getattr(copy, act)()
            else:
                pl.when(used)(getattr(copy, act))

    oa_copy = pltpu.make_async_copy(oa_hbm, o_ref.at[0], o_sem)
    w_copy(0).start()
    oa_copy.start()
    x_copy(0).start()
    run_loads(0, "start")
    oa_copy.wait()
    mc = 1024

    def attend(b):
        run_loads(b, "wait")

        @pl.when(b + 1 < half)
        def _():
            run_loads(b + 1, "start")

        s = lax.rem(b, 2)
        attend_any(me, 4, n_kv, groups, q_buf.at[s], kv_buf.at[s, 0], kv_buf.at[s, 1], kv_buf.at[s, 2], kv_buf.at[s, 3],
                   o_ref.at[1, pl.ds(pl.multiple_of(b * seq, seq), seq)])

    def phase(p):
        @pl.when(p == 1)
        def _():
            pl.loop(0, half)(attend)

        def tile(j):
            t = p * n_tiles + j
            s = lax.rem(t, 2)
            w_copy(t).wait()
            x_copy(t).wait()

            @pl.when(t + 1 < 2 * n_tiles)
            def _():
                w_copy(t + 1).start()
                x_copy(t + 1).start()

            @pl.when(t >= 2)
            def _():
                y_copy(t - 2).wait()

            def rows_step(i):
                acc = cdot(o_ref[p, pl.ds(pl.multiple_of(i * mc, mc), mc), :], w_buf[s])
                to = pl.ds(i * (mc // HD), mc // HD)
                y_buf[s, to] = (x_buf[s, to].astype(F32) + acc.reshape(mc // HD, HD, TN)).astype(BF)

            pl.loop(0, half * seq // mc)(rows_step)
            y_copy(t).start()

        pl.loop(0, n_tiles)(tile)

    pl.loop(0, 2)(phase)
    y_copy(2 * n_tiles - 2).wait()
    y_copy(2 * n_tiles - 1).wait()


def solution(mesh):
    dma = pltpu.SemaphoreType.DMA

    def local_block(hidden, positions, norm_gain, w_query, w_key, w_value, w_out):
        batch, seq, dim = hidden.shape
        heads = w_out.shape[0]
        n_kv = w_key.shape[1] // HD
        first = batch // 2
        nb = 2
        n_chunks = batch // nb
        freq = (10000.0 ** (-2.0 * np.arange(HD // 2, dtype=np.float64) / HD)).astype(np.float32)
        freq = jnp.asarray(np.concatenate([freq, freq])[None, :])
        hbm = pl.BlockSpec(memory_space=pl.ANY)
        vmem = pl.BlockSpec(memory_space=pltpu.VMEM)
        kv_shape = (batch, 2 * n_kv, seq, HD)
        blk = (2 * n_kv, seq, HD)
        shape = jax.ShapeDtypeStruct
        forward_q = ((1, 0), (2, 1), (3, 2), (5, 3), (6, 4))
        forward_a = ((1, 5), (4, 6))
        q, o_first, own, r1, r2, r3 = pl.pallas_call(
            functools.partial(front_kernel, n_kv, first, forward_q, forward_a),
            in_specs=[hbm, vmem, vmem, vmem, hbm, hbm, hbm],
            out_specs=[hbm] * 6,
            out_shape=[
                shape((batch, heads, seq, HD), BF), shape((first * seq, heads * HD), BF),
                shape((batch - first,) + blk, BF), shape(kv_shape, BF), shape(kv_shape, BF), shape(kv_shape, BF)],
            scratch_shapes=[
                pltpu.VMEM((batch * seq, dim), BF), pltpu.VMEM(kv_shape, BF),
                pltpu.VMEM((batch * seq, HD), F32), pltpu.VMEM((batch * seq, HD), F32),
                pltpu.VMEM((2, nb, seq, dim), BF), pltpu.VMEM((3, dim, TN), BF),
                pltpu.VMEM((2, batch, TN // HD, seq, HD), BF),
                pltpu.VMEM((2, heads, seq, HD), BF), pltpu.VMEM((2, 3) + blk, BF), pltpu.VMEM((2, seq, heads * HD), BF),
                dma((2,)), dma((3,)), dma((2,)), dma((2,)), dma((2, 3)), dma((2,)), dma,
            ] + [dma((n_chunks,))] * 6,
            compiler_params=pltpu.CompilerParams(vmem_limit_bytes=VMEM_LIMIT, collective_id=0, has_side_effects=True),
            cost_estimate=pl.CostEstimate(flops=2 * batch * seq * dim * (heads + 2 * n_kv) * HD, bytes_accessed=10 * batch * seq * dim, transcendentals=0),
            name="front",
        )(hidden, positions, norm_gain.reshape(1, dim), freq, w_query, w_key, w_value)
        half = batch - first
        return pl.pallas_call(
            functools.partial(back_kernel, n_kv, first),
            in_specs=[hbm] * 8, out_specs=hbm,
            out_shape=shape((batch, seq, dim), BF),
            scratch_shapes=[
                pltpu.VMEM((2, half * seq, heads * HD), BF), pltpu.VMEM((2, heads * HD, TN), BF),
                pltpu.VMEM((2, half, seq, TN), BF), pltpu.VMEM((2, half, seq, TN), BF),
                pltpu.VMEM((2, heads, seq, HD), BF), pltpu.VMEM((2, 4) + blk, BF),
                dma, dma((2,)), dma((2,)), dma((2,)), dma((2,)), dma((2, 4)),
            ],
            compiler_params=pltpu.CompilerParams(vmem_limit_bytes=VMEM_LIMIT),
            cost_estimate=pl.CostEstimate(flops=2 * batch * seq * dim * heads * HD, bytes_accessed=10 * batch * seq * dim, transcendentals=0),
            name="back",
        )(q, o_first, own, r1, r2, r3, w_out.reshape(heads * HD, dim), hidden)

    act_spec = P('dp', 'cp', None)
    return jax.shard_map(local_block, mesh=mesh, in_specs=(act_spec, P('dp', 'cp'), P(), P(), P(), P(), P()), out_specs=act_spec, check_vma=False)
```

time: 657 us -> 194 us (0.30)
  matrix products: 354 us -> 0 us
  Pallas kernels: 0 us -> 192 us
  waiting for transfers between devices: 134 us -> 0 us
  other arithmetic: 104 us -> 0 us
  local copies, waits for them, and re-layouts: 57.6 us -> 1.3 us
    dot_general x12 -> x0, matrix products: 354 us -> none  [the longest x4 128 us: attend_block(): jnp.einsum('bkgqs,bskd->bkgqd', prob_blk, v_blk, preferred_element_type=j...]
    pallas_call x0 -> x2, Pallas kernels: none -> 192 us  [the longest x1 111 us: local_block(): pl.pallas_call(functools.partial(front_kernel, n_kv, first, forward_q, fo...]
    ppermute x6 -> x0, waiting for transfers between devices: 134 us -> none  [step_fn(): k_blk, v_blk = lax.ppermute((k_blk, v_blk), 'cp', shift_pairs)]
    reduce_sum x5 -> x0, other arithmetic: 60.4 us -> none  [the longest x4 52.3 us: attend_block(): new_sum = run_sum * rescale + jnp.sum(prob_blk, axis=-1)]
    another operation x2 -> x0, local copies, waits for them, and re-layouts: 27.6 us -> none
    concatenate x2 -> x0, other arithmetic: 22 us -> none  [rotary(): jnp.concatenate([first_half * cos_part - second_half * sin_part, second_h...]
    another operation x3 -> x0, other arithmetic: 16.8 us -> none
    while x7 -> x0, local copies, waits for them, and re-layouts: 15.3 us -> none
  transfers between devices with their start and end apart: 6 -> 0, of which waited for: 6 -> 0; matrix products, arithmetic and copies ran while one was open for 0% -> 0% of each run, Pallas kernels for 0% -> 0%
where the time goes in v2:
time: 194 us
  Pallas kernels  192 us (99%)
    pallas_call x1, Pallas kernels, local_block(): pl.pallas_call(functools.partial(front_kernel, n_kv, first, forward_q, fo...  111 us
    pallas_call x1, Pallas kernels, local_block(): pl.pallas_call(functools.partial(back_kernel, n_kv, first), in_specs=[hbm...  81.5 us

profile of v2, /device:TPU:3, one launch (start us, length us, event | category | flops | bytes accessed | tf_op | source)
XLA Modules:
  0.0 194.0 jit_solution(8219369056969456938)
XLA Ops:
  0.0 1.3 reshape.6.gain_ref
  1.3 111.0 %front.1 = (bf16[16,28,128,128]{3,2,1,0:T(8,128)(2,1)}, bf16[1024,3584]{1,0:T(8,128)(2,1)}, bf16[8,8,128,128]{3,2,1,0:T(8,128)(2,1)}, bf16[16,8,128,128]{3,2,1,0...) custom-call(bf16[16,128,3584]{2,1,0:T(8,128)(2,1)} %x_hbm.3, s32[16,128]{1,0:T(8,128)} %pos_ref.1, ...), custom_call_target="tpu_custom_call" | custom-call | flops 67645734912 | bytes 73400320 | tf_op jit(solution)/shard_map/front/pallas_call | solution.py:430
  112.3 81.5 %back.1 = bf16[16,128,3584]{2,1,0:T(8,128)(2,1)} custom-call(bf16[16,28,128,128]{3,2,1,0:T(8,128)(2,1)} %get-tuple-element.11.q_hbm, bf16[1024,3584]{1,0:T(8,128)(2,1)} %get-tuple-element.12.oa_hbm, bf16[8,8,128,128]{3,2,1,0:T(8,128)(2,1)} %get-tuple-element.13.own_hbm, bf16[16,8,128,128]{3,2,1,0:T(8,128)(2,1)} %get-tuple-element.14.r1_hbm, ...), custom_call_target="tpu_custom_call" | custom-call | flops 52613349376 | bytes 73400320 | tf_op jit(solution)/shard_map/back/pallas_call | solution.py:450

commit v3 on v2

--- a/solution.py
+++ b/solution.py
@@ -72,7 +72,7 @@
 def front_kernel(n_kv, n_first, forward_q, forward_a,
                  x_hbm, pos_ref, gain_ref, freq_ref, wq_hbm, wk_hbm, wv_hbm,
                  q_hbm, o_hbm, own_hbm, r1_hbm, r2_hbm, r3_hbm,
-                 h_ref, kv_ref, cos_ref, sin_ref, x_buf, w_buf, q_buf, qa_buf, ra_buf, oa_buf,
+                 h_ref, ha_ref, hb_ref, kv_ref, cos_ref, sin_ref, x_buf, w_buf, q_buf, acc_ref, qa_buf, ra_buf, oa_buf,
                  x_sem, w_sem, q_sem, qa_sem, ra_sem, oa_sem, own_sem,
                  send1, recv1, send2, recv2, send3, recv3):
     batch, seq, dim = x_hbm.shape
@@ -98,9 +98,6 @@
     wv_copy = pltpu.make_async_copy(wv_hbm, w_buf.at[1], w_sem.at[1])
     x_copy(0).start()
     wk_copy.start()
-    wv_copy.start()
-    x_copy(1).start()
-    wq_copy(0).start()
 
     def part(ref, i):
         return ref.at[pl.ds(i * nb, nb)]
@@ -134,7 +131,6 @@
     barrier = pltpu.get_barrier_semaphore()
     for target in (lax.rem(me + 2, 4), me + 1 - 2 * lax.rem(me, 2)):
         pl.semaphore_signal(barrier, inc=1, device_id={"cp": target}, device_id_type=pl.DeviceIdType.MESH)
-    pl.semaphore_wait(barrier, 2)
 
     def send(i):
         @pl.when(low)
@@ -145,34 +141,69 @@
         def _():
             copy2(i).start()
 
+    gain = jnp.concatenate([gain_ref[c:c + 1, :] for c in range(dim // HD)], 1).astype(F32)
+
+    def norm(i, out_ref, part=0, parts=1):
+        n = rows // parts
+        b, r = part * n // seq, part * n % seq
+        if parts == 1:
+            x = x_buf[lax.rem(i, 2)].reshape(rows, dim).astype(F32)
+        else:
+            x = x_buf[lax.rem(i, 2), b, r:r + n].astype(F32)
+        inv = lax.rsqrt(jnp.mean(x * x, axis=-1, keepdims=True) + 1e-5)
+        h = (x * inv * gain).astype(BF)
+        out_ref[part * n:(part + 1) * n] = h
+        h_ref[pl.ds(pl.multiple_of(i * rows + part * n, n), n), :] = h
+
+    x_copy(0).wait()
+    norm(0, ha_ref)
+    x_copy(1).start()
+    wv_copy.start()
+    x_copy(2).start()
     wk_copy.wait()
+    pl.semaphore_wait(barrier, 2)
     wv_copy.wait()
 
-    def kv_chunk(i):
-        x_copy(i).wait()
+    def kv_chunk(i, cur_ref, next_ref):
+        @pl.when(i + 1 < n_chunks)
+        def _():
+            x_copy(i + 1).wait()
+
         at = pl.ds(pl.multiple_of(i * rows, rows), rows)
-        x = x_buf[lax.rem(i, 2)].reshape(rows, dim).astype(F32)
-        inv = lax.rsqrt(jnp.mean(x * x, axis=-1, keepdims=True) + 1e-5)
-        h = (x * inv * gain_ref[...].astype(F32)).astype(BF)
-        h_ref[at, :] = h
         cos, sin = cos_ref[at, :], sin_ref[at, :]
-        k = cdot(h, w_buf[0])
         to = pl.ds(i * nb, nb)
-        for n in range(n_kv):
-            kv_ref[to, n] = rope_tile(k[:, n * HD:(n + 1) * HD], cos, sin).astype(BF).reshape(nb, seq, HD)
-        v = cdot(h, w_buf[1]).astype(BF)
-        for n in range(n_kv):
-            kv_ref[to, n_kv + n] = v[:, n * HD:(n + 1) * HD].reshape(nb, seq, HD)
-
-        @pl.when(i + 2 < n_chunks)
-        def _():
-            x_copy(i + 2).start()
+        parts = 4
+        width = n_kv * HD
+        step = 2 * width // parts
+        for c in range(parts):
+            col = c * step
+            w = w_buf[col // width, :, col % width:col % width + step]
+            acc = cdot(cur_ref[...], w)
+            norm(i + 1, next_ref, c, parts)
+            for n in range(step // HD):
+                t = acc[:, n * HD:(n + 1) * HD]
+                if col < width:
+                    t = rope_tile(t, cos, sin)
+                kv_ref[to, col // HD + n] = t.astype(BF).reshape(nb, seq, HD)
+
+        @pl.when(i + 3 < n_chunks)
+        def _():
+            x_copy(i + 3).start()
 
         @pl.when(i > 0)
         def _():
             send(i - 1)
 
-    pl.loop(0, n_chunks)(kv_chunk)
+    def kv_pair(i):
+        kv_chunk(2 * i, ha_ref, hb_ref)
+
+        @pl.when(i == 0)
+        def _():
+            wq_copy(0).start()
+
+        kv_chunk(2 * i + 1, hb_ref, ha_ref)
+
+    pl.loop(0, n_chunks // 2)(kv_pair)
     wq_copy(1).start()
 
     def forward(i):
@@ -182,11 +213,19 @@
             copy3(i).start()
 
     def q_copy(j):
-        s = lax.rem(j, 2)
+        s = lax.rem(j, 3)
         return pltpu.make_async_copy(q_buf.at[s], q_hbm.at[:, pl.ds(j * tile_heads, tile_heads)], q_sem.at[s])
 
     own_copy = pltpu.make_async_copy(kv_ref.at[pl.ds(n_first, batch - n_first)], own_hbm, own_sem)
-    mc = 1024
+    mc = acc_ref.shape[1]
+    n_parts = batch * seq // mc
+
+    def finish_part(i, slot):
+        at = slice(i * mc, (i + 1) * mc)
+        cos, sin = cos_ref[at, :], sin_ref[at, :]
+        for n in range(tile_heads):
+            t = rope_tile(acc_ref[i % 2, :, n * HD:(n + 1) * HD], cos, sin).astype(BF)
+            q_buf[slot, i * (mc // HD):(i + 1) * (mc // HD), n] = t.reshape(mc // HD, HD, HD)
 
     def q_tile(j):
         @pl.when(j == 0)
@@ -205,26 +244,27 @@
         def _():
             wq_copy(j + 1).start()
 
-        @pl.when(j >= 2)
-        def _():
-            q_copy(j - 2).wait()
-
-        ws, qs = lax.rem(j + 2, 3), lax.rem(j, 2)
-
-        def rows_step(i):
-            at = pl.ds(pl.multiple_of(i * mc, mc), mc)
-            acc = cdot(h_ref[at, :], w_buf[ws])
-            cos, sin = cos_ref[at, :], sin_ref[at, :]
-            for n in range(tile_heads):
-                t = rope_tile(acc[:, n * HD:(n + 1) * HD], cos, sin).astype(BF)
-                q_buf[qs, pl.ds(i * (mc // HD), mc // HD), n] = t.reshape(mc // HD, HD, HD)
-
-        pl.loop(0, batch * seq // mc)(rows_step)
-        q_copy(j).start()
+        @pl.when(j >= 3)
+        def _():
+            q_copy(j - 3).wait()
+
+        ws, qs, before = lax.rem(j + 2, 3), lax.rem(j, 3), lax.rem(j + 2, 3)
+        for i in range(n_parts):
+            acc_ref[i % 2] = cdot(h_ref[i * mc:(i + 1) * mc, :], w_buf[ws])
+            if i == 0:
+                finish_part(n_parts - 1, before)
+            else:
+                finish_part(i - 1, qs)
+
+        @pl.when(j > 0)
+        def _():
+            q_copy(j - 1).start()
 
     pl.loop(0, n_tiles)(q_tile)
-    q_copy(n_tiles - 2).wait()
-    q_copy(n_tiles - 1).wait()
+    finish_part(n_parts - 1, (n_tiles - 1) % 3)
+    q_copy(n_tiles - 1).start()
+    for j in range(n_tiles - 3, n_tiles):
+        q_copy(j).wait()
 
     first_chunks = n_first // nb
     for i in range(first_chunks):
@@ -325,20 +365,20 @@
     me = lax.axis_index("cp")
     high, odd = me >= 2, lax.rem(me, 2) == 1
 
-    def w_copy(t):
-        s = lax.rem(t, 2)
-        col = pl.multiple_of(lax.rem(t, n_tiles) * TN, TN)
-        return pltpu.make_async_copy(w_hbm.at[:, pl.ds(col, TN)], w_buf.at[s], w_sem.at[s])
-
-    def x_copy(t):
-        s = lax.rem(t, 2)
-        col = pl.multiple_of(lax.rem(t, n_tiles) * TN, TN)
-        return pltpu.make_async_copy(x_hbm.at[pl.ds(lax.div(t, n_tiles) * half, half), :, pl.ds(col, TN)], x_buf.at[s], x_sem.at[s])
-
-    def y_copy(t):
-        s = lax.rem(t, 2)
-        col = pl.multiple_of(lax.rem(t, n_tiles) * TN, TN)
-        return pltpu.make_async_copy(y_buf.at[s], y_hbm.at[pl.ds(lax.div(t, n_tiles) * half, half), :, pl.ds(col, TN)], y_sem.at[s])
+    def cols(j):
+        return pl.ds(pl.multiple_of(j * TN, TN), TN)
+
+    def w_copy(j):
+        s = lax.rem(j, 2)
+        return pltpu.make_async_copy(w_hbm.at[:, cols(j)], w_buf.at[s], w_sem.at[s])
+
+    def x_copy(j):
+        s = lax.rem(j, 2)
+        return pltpu.make_async_copy(x_hbm.at[:, :, cols(j)], x_buf.at[s], x_sem.at[s])
+
+    def y_copy(j):
+        s = lax.rem(j, 2)
+        return pltpu.make_async_copy(y_buf.at[s], y_hbm.at[:, :, cols(j)], y_sem.at[s])
 
     def loads(b):
         s = lax.rem(b, 2)
@@ -354,13 +394,9 @@
             else:
                 pl.when(used)(getattr(copy, act))
 
-    oa_copy = pltpu.make_async_copy(oa_hbm, o_ref.at[0], o_sem)
-    w_copy(0).start()
-    oa_copy.start()
-    x_copy(0).start()
+    oa_copy = pltpu.make_async_copy(oa_hbm, o_ref.at[pl.ds(0, n_first * seq)], o_sem)
     run_loads(0, "start")
-    oa_copy.wait()
-    mc = 1024
+    mc = 2048
 
     def attend(b):
         run_loads(b, "wait")
@@ -369,43 +405,44 @@
         def _():
             run_loads(b + 1, "start")
 
+        @pl.when(b == 0)
+        def _():
+            oa_copy.start()
+            w_copy(0).start()
+            x_copy(0).start()
+
         s = lax.rem(b, 2)
         attend_any(me, 4, n_kv, groups, q_buf.at[s], kv_buf.at[s, 0], kv_buf.at[s, 1], kv_buf.at[s, 2], kv_buf.at[s, 3],
-                   o_ref.at[1, pl.ds(pl.multiple_of(b * seq, seq), seq)])
-
-    def phase(p):
-        @pl.when(p == 1)
-        def _():
-            pl.loop(0, half)(attend)
-
-        def tile(j):
-            t = p * n_tiles + j
-            s = lax.rem(t, 2)
-            w_copy(t).wait()
-            x_copy(t).wait()
-
-            @pl.when(t + 1 < 2 * n_tiles)
-            def _():
-                w_copy(t + 1).start()
-                x_copy(t + 1).start()
-
-            @pl.when(t >= 2)
-            def _():
-                y_copy(t - 2).wait()
-
-            def rows_step(i):
-                acc = cdot(o_ref[p, pl.ds(pl.multiple_of(i * mc, mc), mc), :], w_buf[s])
-                to = pl.ds(i * (mc // HD), mc // HD)
-                y_buf[s, to] = (x_buf[s, to].astype(F32) + acc.reshape(mc // HD, HD, TN)).astype(BF)
-
-            pl.loop(0, half * seq // mc)(rows_step)
-            y_copy(t).start()
-
-        pl.loop(0, n_tiles)(tile)
-
-    pl.loop(0, 2)(phase)
-    y_copy(2 * n_tiles - 2).wait()
-    y_copy(2 * n_tiles - 1).wait()
+                   o_ref.at[pl.ds(pl.multiple_of((n_first + b) * seq, seq), seq)])
+
+    pl.loop(0, half)(attend)
+    oa_copy.wait()
+
+    def tile(j):
+        s = lax.rem(j, 2)
+        w_copy(j).wait()
+        x_copy(j).wait()
+
+        @pl.when(j + 1 < n_tiles)
+        def _():
+            w_copy(j + 1).start()
+            x_copy(j + 1).start()
+
+        @pl.when(j >= 2)
+        def _():
+            y_copy(j - 2).wait()
+
+        def rows_step(i):
+            acc = cdot(o_ref[pl.ds(pl.multiple_of(i * mc, mc), mc), :], w_buf[s])
+            to = pl.ds(i * (mc // HD), mc // HD)
+            y_buf[s, to] = (x_buf[s, to].astype(F32) + acc.reshape(mc // HD, HD, TN)).astype(BF)
+
+        pl.loop(0, batch * seq // mc)(rows_step)
+        y_copy(j).start()
+
+    pl.loop(0, n_tiles)(tile)
+    y_copy(n_tiles - 2).wait()
+    y_copy(n_tiles - 1).wait()
 
 
 def solution(mesh):
@@ -435,25 +472,25 @@
                 shape((batch, heads, seq, HD), BF), shape((first * seq, heads * HD), BF),
                 shape((batch - first,) + blk, BF), shape(kv_shape, BF), shape(kv_shape, BF), shape(kv_shape, BF)],
             scratch_shapes=[
-                pltpu.VMEM((batch * seq, dim), BF), pltpu.VMEM(kv_shape, BF),
+                pltpu.VMEM(((batch + nb) * seq, dim), BF), pltpu.VMEM((nb * seq, dim), BF), pltpu.VMEM((nb * seq, dim), BF), pltpu.VMEM(kv_shape, BF),
                 pltpu.VMEM((batch * seq, HD), F32), pltpu.VMEM((batch * seq, HD), F32),
                 pltpu.VMEM((2, nb, seq, dim), BF), pltpu.VMEM((3, dim, TN), BF),
-                pltpu.VMEM((2, batch, TN // HD, seq, HD), BF),
+                pltpu.VMEM((3, batch, TN // HD, seq, HD), BF), pltpu.VMEM((2, 512, TN), F32),
                 pltpu.VMEM((2, heads, seq, HD), BF), pltpu.VMEM((2, 3) + blk, BF), pltpu.VMEM((2, seq, heads * HD), BF),
-                dma((2,)), dma((3,)), dma((2,)), dma((2,)), dma((2, 3)), dma((2,)), dma,
+                dma((2,)), dma((3,)), dma((3,)), dma((2,)), dma((2, 3)), dma((2,)), dma,
             ] + [dma((n_chunks,))] * 6,
             compiler_params=pltpu.CompilerParams(vmem_limit_bytes=VMEM_LIMIT, collective_id=0, has_side_effects=True),
             cost_estimate=pl.CostEstimate(flops=2 * batch * seq * dim * (heads + 2 * n_kv) * HD, bytes_accessed=10 * batch * seq * dim, transcendentals=0),
             name="front",
-        )(hidden, positions, norm_gain.reshape(1, dim), freq, w_query, w_key, w_value)
+        )(hidden, positions, norm_gain.reshape(dim // HD, HD), freq, w_query, w_key, w_value)
         half = batch - first
         return pl.pallas_call(
             functools.partial(back_kernel, n_kv, first),
             in_specs=[hbm] * 8, out_specs=hbm,
             out_shape=shape((batch, seq, dim), BF),
             scratch_shapes=[
-                pltpu.VMEM((2, half * seq, heads * HD), BF), pltpu.VMEM((2, heads * HD, TN), BF),
-                pltpu.VMEM((2, half, seq, TN), BF), pltpu.VMEM((2, half, seq, TN), BF),
+                pltpu.VMEM((batch * seq, heads * HD), BF), pltpu.VMEM((2, heads * HD, TN), BF),
+                pltpu.VMEM((2, batch, seq, TN), BF), pltpu.VMEM((2, batch, seq, TN), BF),
                 pltpu.VMEM((2, heads, seq, HD), BF), pltpu.VMEM((2, 4) + blk, BF),
                 dma, dma((2,)), dma((2,)), dma((2,)), dma((2,)), dma((2, 4)),
             ],

time: 194 us -> 188 us (0.969)
  Pallas kernels: 192 us -> 187 us
    pallas_call x1, Pallas kernels: 111 us -> 108 us  [local_block(): pl.pallas_call(functools.partial(front_kernel, n_kv, first, forward_q, fo...]
    pallas_call x1, Pallas kernels: 81.5 us -> 79 us  [local_block(): pl.pallas_call(functools.partial(back_kernel, n_kv, first), in_specs=[hbm...]
where the time goes in v3:
time: 188 us
  Pallas kernels  187 us (99%)
    pallas_call x1, Pallas kernels, local_block(): pl.pallas_call(functools.partial(front_kernel, n_kv, first, forward_q, fo...  108 us
    pallas_call x1, Pallas kernels, local_block(): pl.pallas_call(functools.partial(back_kernel, n_kv, first), in_specs=[hbm...  79 us

profile of v3, /device:TPU:3, one launch (start us, length us, event | category | flops | bytes accessed | tf_op | source)
XLA Modules:
  0.0 187.7 jit_solution(13388626172126586771)
XLA Ops:
  0.0 108.4 %front.1 = (bf16[16,28,128,128]{3,2,1,0:T(8,128)(2,1)}, bf16[1024,3584]{1,0:T(8,128)(2,1)}, bf16[8,8,128,128]{3,2,1,0:T(8,128)(2,1)}, bf16[16,8,128,128]{3,2,1,0...) custom-call(bf16[16,128,3584]{2,1,0:T(8,128)(2,1)} %x_hbm.3, s32[16,128]{1,0:T(8,128)} %pos_ref.1, ...), custom_call_target="tpu_custom_call" | custom-call | flops 67645734912 | bytes 73400320 | tf_op jit(solution)/shard_map/front/pallas_call | solution.py:467
  108.4 79.0 %back.1 = bf16[16,128,3584]{2,1,0:T(8,128)(2,1)} custom-call(bf16[16,28,128,128]{3,2,1,0:T(8,128)(2,1)} %get-tuple-element.11.q_hbm, bf16[1024,3584]{1,0:T(8,128)(2,1)} %get-tuple-element.12.oa_hbm, bf16[8,8,128,128]{3,2,1,0:T(8,128)(2,1)} %get-tuple-element.13.own_hbm, bf16[16,8,128,128]{3,2,1,0:T(8,128)(2,1)} %get-tuple-element.14.r1_hbm, ...), custom_call_target="tpu_custom_call" | custom-call | flops 52613349376 | bytes 73400320 | tf_op jit(solution)/shard_map/back/pallas_call | solution.py:487
